TPU v7x, 256 devices: a 4x2x16 block of a 4x16x16 slice. The times are simulated.
256 devices in a mesh: rep: 2 (over y), tp: 32 (over z, core), sub: 4 (over x).
Axes of the slice: x: 4, y: 2, z: 16, core: 2. Of those that a mesh axis runs over, the one named last changes fastest.
The devices are a block of a 4x16x16 slice.
Arguments:
- hidden_in: bfloat16 [128, 6144], P(('rep', 'sub'), 'tp'), parts along dimension 0, may hold values from -128 to 128
- query: bfloat16 [128, 6144], P(('rep', 'sub'), 'tp'), parts along dimension 0, may hold values from -128 to 128
- key_new: bfloat16 [128, 1024], P(('rep', 'sub'), 'tp'), parts along dimension 0, may hold values from -8 to 8
- value_new: bfloat16 [128, 1024], P(('rep', 'sub'), 'tp'), parts along dimension 0, may hold values from -6 to 6
- key_cache: bfloat16 [128, 1024, 1024], P(('rep', 'sub'), 'tp'), parts along dimension 0, may hold values from -8 to 8
- value_cache: bfloat16 [128, 1024, 1024], P(('rep', 'sub'), 'tp'), parts along dimension 0, may hold values from -6 to 6
- lengths: int32 [128], P(('rep', 'sub')), parts along dimension 0, may hold values from 2 to 1024
- out_weight: bfloat16 [6144, 6144], P('sub', 'tp'), may hold values from -0.078125 to 0.078125
- norm_gain: bfloat16 [6144], P('tp'), may hold values from 0.099609375 to 1.8984375
- router_weight: bfloat16 [6144, 4], P('tp'), may hold values from -0.078125 to 0.078125
- routes: int32 [128, 2], P(('rep', 'sub')), parts along dimension 0, may hold values from 0 to 3, all different within a row; in each aligned block of 16 rows (0 to 15, 16 to 31, ...) at most 12 rows name the same one
- gate_weight: bfloat16 [4, 6144, 8192], P('sub', None, 'tp'), may hold values from -0.078125 to 0.078125
- up_weight: bfloat16 [4, 6144, 8192], P('sub', None, 'tp'), may hold values from -0.078125 to 0.078125
- down_weight: bfloat16 [4, 8192, 6144], P('sub', 'tp'), may hold values from -0.125 to 0.125
Outputs:
- layer_out: bfloat16 [128, 6144], P(('rep', 'sub'), 'tp'), parts along dimension 0
There are 2 independent parts, one for each index of `rep`. A program takes and returns all parts, laid end to end along the dimension named above; an argument that names none is the same for every part. Nothing has to cross between parts.
Inputs may be any that keep to these rules, and one draw needn't show every extreme that they name: `routes`: the two experts of a row differ; within the 16 rows of one index of sub, no expert is named by more than 12 rows, a bound that some such block reaches.
All inputs are finite; a program needn't handle non-finite values.
Results may differ from a plain program's by a relative error of at most 0.0075.
Values may be sent and summed in bfloat16 or wider, within the bound.
A program may use at most 128 MiB of HBM per device.

v0:
```python
import jax
import jax.numpy as jnp
from jax import lax
from jax.sharding import Mesh
from jax.sharding import PartitionSpec as P

D = 6144
H = 48
KVH = 8
HD = 128
E = 4
MOST = 12
TP = ("tp_0", "tp_1")


def side_by_side(arrays, axis, dim, along):
    ends, at = ([], 0)
    for a in arrays[:-1]:
        at += a.shape[along]
        ends.append(at)
    both = jnp.concatenate(arrays, axis=along)
    return tuple(jnp.split(lax.all_gather(both, axis, axis=dim, tiled=True), ends, axis=along))


def combined_by_axis(value, axes, combine):
    for axis in axes:
        pieces = jax.tree.map(lambda part: lax.all_gather(part, axis), value)
        value = jax.tree.map(lambda part: part[0], pieces)
        for k in range(1, lax.axis_size(axis)):
            value = combine(value, jax.tree.map(lambda part: part[k], pieces))
    return value


def in_order(parts, dim):
    parts = jnp.moveaxis(parts, 0, dim)
    dims = parts.shape
    return parts.reshape(*dims[:dim], dims[dim] * dims[dim + 1], *dims[dim + 2 :])


def sent_to_all(value, axis):
    count = lax.axis_size(axis)
    return lax.all_to_all(
        jnp.broadcast_to(value[None], (count, *value.shape)), axis, 0, 0, tiled=True
    )


def gathered_copies(value, axis, dim):
    return in_order(sent_to_all(value, axis), dim)


def taken_together(value, axis):
    return sent_to_all(value, axis).sum(axis=0)


def all_blocks(value, axes, order):
    parts = value
    for k in order:
        parts = lax.all_gather(parts, axes[k])
    done = order[::-1]
    back = [done.index(k) for k in range(len(axes))]
    parts = parts.transpose(*back, *range(len(axes), parts.ndim))
    return parts.reshape(-1, *value.shape)


def gather_axes(value, axes, order, dim):
    return in_order(all_blocks(value, axes, order), dim)


def in_blocks(value, dim, count):
    dims = value.shape
    parts = value.reshape(*dims[:dim], count, dims[dim] // count, *dims[dim + 1 :])
    return jnp.moveaxis(parts, dim, 0)


def summed_on_arrival(value, axis, dim):
    count = lax.axis_size(axis)
    parts = lax.all_to_all(in_blocks(value, dim, count), axis, 0, 0, tiled=True)
    return jnp.sum(parts, axis=0)


def join_softmax(first, second):
    joined = jnp.maximum(first[0], second[0])
    first_scale = jnp.exp(first[0] - joined)
    second_scale = jnp.exp(second[0] - joined)
    totals = first[1] * first_scale + second[1] * second_scale
    summed = first[2] * first_scale[..., None] + second[2] * second_scale[..., None]
    return (joined, totals, summed)


def on_device(
    hidden_in,
    query,
    key_new,
    value_new,
    key_cache,
    value_cache,
    lengths,
    out_weight,
    norm_gain,
    router_weight,
    routes,
    gate_weight,
    up_weight,
    down_weight,
):
    seq_rows = hidden_in.shape[0]
    group_size = H // KVH
    scale_factor = 1.0 / HD**0.5
    local_len = key_cache.shape[1]
    all_query, all_key, all_value = (
        lax.all_gather(query, TP, axis=1, tiled=True),
        *side_by_side((key_new, value_new), TP, 1, 0),
    )
    query_rows = all_query.reshape(seq_rows, KVH, group_size, HD)
    cached_keys = key_cache.reshape(seq_rows, local_len, KVH, HD)
    cached_values = value_cache.reshape(seq_rows, local_len, KVH, HD).astype(jnp.float32)
    scores = (
        jnp.einsum("bkgd,bpkd->bkgp", query_rows, cached_keys, preferred_element_type=jnp.float32)
        * scale_factor
    )
    positions = lax.axis_index(TP) * local_len + jnp.arange(local_len, dtype=jnp.int32)
    valid = positions[None, :] < lengths[:, None]
    scores = jnp.where(valid[:, None, None, :], scores, -jnp.inf)
    owned_part = (
        jnp.einsum(
            "zyqn,zyn->zyq",
            query_rows,
            all_key.reshape(seq_rows, KVH, HD),
            preferred_element_type=jnp.float32,
        )
        * scale_factor
    )
    local_max = jnp.maximum(jnp.max(scores, axis=-1), owned_part)
    weights = jnp.exp(scores - local_max[..., None])
    partial_total = jnp.sum(weights, axis=-1)
    local_summed = jnp.einsum("bkgp,bpkd->bkgd", weights, cached_values)
    run_max, total, summed = combined_by_axis(
        (local_max, partial_total, local_summed), TP, join_softmax
    )
    own_weight = jnp.exp(owned_part - run_max)
    total = total + own_weight
    new_values = all_value.reshape(seq_rows, KVH, 1, HD).astype(jnp.float32)
    summed = summed + own_weight[..., None] * new_values
    attn = (summed / total[..., None]).reshape(seq_rows, H * HD).astype(jnp.bfloat16)
    column_span = attn
    projected = jnp.dot(
        column_span, gathered_copies(out_weight, "sub", 0), preferred_element_type=jnp.float32
    )
    resid = hidden_in.astype(jnp.float32) + projected
    gain_full = norm_gain.astype(jnp.float32)[None, :]
    router_full = router_weight.astype(jnp.float32)
    squares = taken_together(jnp.sum(resid * resid, axis=-1), TP)
    root = jnp.sqrt(squares / D + 1e-05)
    normed = resid / root[:, None] * gain_full
    logits = taken_together(jnp.dot(normed, router_full), TP)
    normed_low = normed.astype(jnp.bfloat16)
    expert_ids = jnp.arange(E, dtype=jnp.int32)[None, :]
    first_hot = (routes[:, 0:1] == expert_ids).astype(jnp.float32)
    second_hot = (routes[:, 1:2] == expert_ids).astype(jnp.float32)
    first_logit = jnp.sum(logits * first_hot, axis=-1)
    second_logit = jnp.sum(logits * second_hot, axis=-1)
    first_weight = 1.0 / (1.0 + jnp.exp(second_logit - first_logit))
    second_weight = 1.0 / (1.0 + jnp.exp(first_logit - second_logit))
    dense = first_weight[:, None] * first_hot + second_weight[:, None] * second_hot
    gate_local = gate_weight[0]
    up_local = up_weight[0]
    down_local = down_weight[0]
    routed_mask = first_hot + second_hot
    rank = jnp.cumsum(routed_mask, axis=0) - routed_mask
    slot_ids = jnp.arange(MOST, dtype=jnp.float32)
    selector = routed_mask.T[:, None, :] * (rank.T[:, None, :] == slot_ids[None, :, None]).astype(
        jnp.float32
    )
    send_rows = jnp.einsum(
        "emb,bc->emc", selector.astype(jnp.bfloat16), normed_low, preferred_element_type=jnp.float32
    ).astype(jnp.bfloat16)
    received = lax.all_to_all(send_rows, "sub", split_axis=0, concat_axis=0, tiled=True)
    sources, slots, column_span = received.shape
    piece = gather_axes(received.reshape(sources * slots, column_span), TP, (0, 1), 1)
    gate_out = jnp.dot(piece, gate_local, preferred_element_type=jnp.float32)
    up_out = jnp.dot(piece, up_local, preferred_element_type=jnp.float32)
    inner = (jax.nn.silu(gate_out) * up_out).astype(jnp.bfloat16)
    result = jnp.dot(inner, down_local, preferred_element_type=jnp.float32)
    outputs = summed_on_arrival(result, TP, 1).reshape(sources, slots, column_span)
    returned = lax.all_to_all(outputs, "sub", split_axis=0, concat_axis=0, tiled=True)
    weighted = selector * dense.T[:, None, :]
    mixed = jnp.einsum("emb,emc->bc", weighted, returned)
    return (resid + mixed).astype(jnp.bfloat16)


def solution(mesh):
    split = Mesh(
        mesh.devices.reshape(mesh.shape["rep"], 16, 2, mesh.shape["sub"]),
        ("rep", "tp_0", "tp_1", "sub"),
    )
    return jax.shard_map(
        on_device,
        mesh=split,
        in_specs=(
            P(("rep", "sub"), TP),
            P(("rep", "sub"), TP),
            P(("rep", "sub"), TP),
            P(("rep", "sub"), TP),
            P(("rep", "sub"), TP, None),
            P(("rep", "sub"), TP, None),
            P(("rep", "sub")),
            P("sub", TP),
            P(TP),
            P(TP, None),
            P(("rep", "sub"), None),
            P("sub", None, TP),
            P("sub", None, TP),
            P("sub", TP, None),
        ),
        out_specs=P(("rep", "sub"), TP),
        check_vma=False,
    )
```

profile of v0, /device:TPU:33, one launch (start us, length us, event | category | flops | bytes accessed | tf_op | source)
XLA Modules:
  0.0 522.4 jit_solution(8818489390149967905)
XLA Ops:
  6.6 51.5 %all-gather.4 = bf16[32,192,16]{1,2,0:T(8,128)(2,1)S(1)} all-gather(bf16[1,192,16]{1,2,0:T(8,128)(2,1)} %bitcast.708), channel_id=1, replica_groups=mesh['rep'=2,'tp_0'=16,'tp_1'=2,'sub'=4] {'tp_0','tp_1'}, dimensions={0}, use_global_device_ids=true | all-gather | bytes 202752 | tf_op jit(solution)/shard_map/all_gather | solution.py:111
  59.1 1.9 reshape.1214
  62.7 27.9 %all_gather.46 = bf16[32,1024]{0,1:T(8,128)(2,1)S(1)} all-gather(bf16[32,32]{0,1:T(8,128)(2,1)S(1)} %pad_maximum_fusion), channel_id=1, replica_groups=mesh['rep'=2,'tp_0'=16,'tp_1'=2,'sub'=4] {'tp_0','tp_1'}, dimensions={1}, use_global_device_ids=true | all-gather | bytes 67584 | tf_op jit(solution)/shard_map/all_gather | solution.py:22
  93.8 2.1 fusion.172
  96.6 1.7 fusion.16
  99.2 2.7 broadcast_in_dim.20
  101.9 4.6 all-to-all-start
  106.5 40.6 %all-gather.1 = f32[256,8,6]{2,1,0:T(8,128)S(1)} all-gather(f32[16,8,6]{2,1,0:T(8,128)S(1)} %multiply_maximum_fusion), channel_id=3, replica_groups=mesh['rep'=2,'tp_0'=16,'tp_1'=2,'sub'=4] {'tp_0'}, dimensions={0}, use_global_device_ids=true | all-gather | bytes 52224 | tf_op jit(solution)/shard_map/all_gather | solution.py:27
  171.5 6.8 %all_gather.52 = f32[2,16,8,6]{1,2,3,0:T(8,128)S(1)} all-gather(f32[1,16,8,6]{1,2,3,0:T(8,128)S(1)} %bitcast_maximum_fusion.1), channel_id=1, replica_groups=mesh['rep'=2,'tp_0'=16,'tp_1'=2,'sub'=4] {'tp_1'}, dimensions={0}, use_global_device_ids=true | all-gather | bytes 9216 | tf_op jit(solution)/shard_map/all_gather | solution.py:27
  183.3 26.0 %all-gather.2 = f32[256,8,6]{2,1,0:T(8,128)S(1)} all-gather(f32[16,8,6]{2,1,0:T(8,128)S(1)} %fusion.23), channel_id=4, replica_groups=mesh['rep'=2,'tp_0'=16,'tp_1'=2,'sub'=4] {'tp_0'}, dimensions={0}, use_global_device_ids=true | all-gather | bytes 52224 | tf_op jit(solution)/shard_map/all_gather | solution.py:27
  236.5 8.5 %all_gather.55 = f32[2,16,8,6]{1,2,3,0:T(8,128)S(1)} all-gather(f32[1,16,8,6]{1,2,3,0:T(8,128)S(1)} %fusion.88), channel_id=1, replica_groups=mesh['rep'=2,'tp_0'=16,'tp_1'=2,'sub'=4] {'tp_1'}, dimensions={0}, use_global_device_ids=true | all-gather | bytes 9216 | tf_op jit(solution)/shard_map/all_gather | solution.py:27
  248.6 1.7 fusion.77
  250.3 1.6 copy.372
  253.6 1.6 copy.374
  255.2 1.6 copy.394
  310.3 3.5 copy.448
  313.8 7.3 %fusion.30 = f32[1,16,8,6,128]{4,2,3,1,0:T(8,128)S(1)} fusion(f32[256,8,6,128]{3,1,2,0:T(8,128)} %all-gather.7.cloned.1.call-done, f32[16,8,6]{1,2,0:T(8,128)S(1)} %copy-done.6, f32[16,8,6]{1,2,0:T(8,128)S(1)} %copy-done.5, f32[16,8,6]{1,2,0:T(8,128)S(1)} %copy-done.4, f32[16,8,6]{1,2,0:T(8,128)S(1)} %copy.365, f32[16,8,6]{1,2,0:T(8,128)S(1)} %copy.363, ...), kind=kLoop, calls=%fused_computation.31 | loop fusion | flops 4423680 | bytes 6776832 | tf_op jit(solution)/shard_map/add | solution.py:86
  321.2 2.6 all_gather.51
  325.3 2.6 multiply_reduce_fusion
  328.6 6.7 %all-to-all-start.1 = ((f32[32,1,16]{2,1,0:T(1,128)}), f32[32,1,16]{2,1,0:T(1,128)S(1)}, u32[]{:S(2)}, u32[]{:S(2)}) async-start(f32[32,1,16]{2,1,0:T(1,128)} %broadcast_in_dim.21), calls=%async_computation.1 | async-start | bytes 32768 | tf_op jit(solution)/shard_map/all_to_all | solution.py:42
  335.2 11.6 %all-to-all-done.1 = f32[32,1,16]{2,1,0:T(1,128)S(1)} async-done(((f32[32,1,16]{2,1,0:T(1,128)}), f32[32,1,16]{2,1,0:T(1,128)S(1)}, u32[]{:S(2)}, u32[]{:S(2)}) %all-to-all-start.1) | async-done | bytes 2080 | tf_op jit(solution)/shard_map/all_to_all | solution.py:42
  347.7 4.6 all-to-all-start.2
  352.4 13.4 %all-to-all-done.2 = f32[32,16,4]{1,2,0:T(4,128)S(1)} async-done(((f32[32,16,4]{1,2,0:T(4,128)}), f32[32,16,4]{1,2,0:T(4,128)S(1)}, u32[]{:S(2)}, u32[]{:S(2)}) %all-to-all-start.2) | async-done | bytes 8224 | tf_op jit(solution)/shard_map/all_to_all | solution.py:42
  367.1 4.6 all-to-all-start.3
  371.7 4.7 copy.405
  376.4 21.5 %all_gather.56 = bf16[16,48,192]{2,1,0:T(8,128)(2,1)S(1)} all-gather(bf16[1,48,192]{2,1,0:T(8,128)(2,1)S(1)} %all_gather_reshape.3), channel_id=1, replica_groups=mesh['rep'=2,'tp_0'=16,'tp_1'=2,'sub'=4] {'tp_0'}, dimensions={0}, use_global_device_ids=true | all-gather | bytes 313344 | tf_op jit(solution)/shard_map/all_gather | solution.py:58
  397.9 11.6 %all-gather.3 = bf16[32,48,192]{2,1,0:T(8,128)(2,1)S(1)} all-gather(bf16[16,48,192]{2,1,0:T(8,128)(2,1)S(1)} %all_gather.56), channel_id=5, replica_groups=mesh['rep'=2,'tp_0'=16,'tp_1'=2,'sub'=4] {'tp_1'}, dimensions={0}, use_global_device_ids=true | all-gather | bytes 884736 | tf_op jit(solution)/shard_map/all_gather | solution.py:58
  410.8 2.6 reshape.1220
  413.3 2.7 fusion.2
  416.1 5.6 %convolution_bitcast_fusion = f32[32,48,192]{2,1,0:T(8,128)} fusion(bf16[32,192,256]{2,1,0:T(8,128)(2,1)} %bitcast.699, bf16[48,6144]{1,0:T(8,128)(2,1)} %reshape.1220, bf16[1,6144,256]{2,1,0:T(8,128)(2,1)S(1)} %copy-done, f32[48,256]{1,0:T(8,128)S(1)} %fusion.2), kind=kOutput, calls=%fused_computation.4 | convolution fusion | flops 302063616 | bytes 8110080 | tf_op jit(solution)/shard_map/dot_general | solution.py:183
  421.6 83.6 %all_to_all.31 = f32[32,48,192]{2,1,0:T(8,128)} all-to-all(f32[32,48,192]{2,1,0:T(8,128)} %convolution_bitcast_fusion), channel_id=1, replica_groups=mesh['rep'=2,'tp_0'=16,'tp_1'=2,'sub'=4] {'tp_0','tp_1'}, dimensions={0} | all-to-all | bytes 2359296 | tf_op jit(solution)/shard_map/all_to_all | solution.py:77
  506.8 8.0 %all_to_all.32 = bf16[4,12,192]{2,1,0:T(8,128)(2,1)S(1)} all-to-all(bf16[4,12,192]{2,1,0:T(8,128)(2,1)S(1)} %reshape.1221), channel_id=1, replica_groups=mesh['rep'=2,'tp_0'=16,'tp_1'=2,'sub'=4] {'sub'}, dimensions={0} | all-to-all | bytes 36864 | tf_op jit(solution)/shard_map/all_to_all | solution.py:185
  (165 shorter events, 130.7 us)
Async XLA Ops:
  6.5 409.5 %copy-start = (bf16[1,6144,256]{2,1,0:T(8,128)(2,1)S(1)}, bf16[1,6144,256]{2,1,0:T(8,128)(2,1)}, u32[]{:S(2)}) copy-start(bf16[1,6144,256]{2,1,0:T(8,128)(2,1)} %param.26) | copy-start | bytes 9437188
  6.6 85.9 %copy-start.16 = (s32[16]{0:T(128)S(1)}, s32[16]{0:T(128)}, u32[]{:S(2)}) copy-start(s32[16]{0:T(128)} %param.20) | copy-start | bytes 196
  6.6 307.2 %all-gather.7.cloned.1.call-start = ((), (), s32[]{:S(2)}) async-start(), calls=%async_computation.6 | async-start | bytes 6684672 | tf_op jit(solution)/shard_map/all_gather | solution.py:27
  93.8 2.1 copy-start.8
  95.8 0.8 copy-start.1
  101.9 208.4 %all-to-all-start = ((bf16[4,1536,192]{1,2,0:T(8,128)(2,1)}), bf16[4,1536,192]{1,2,0:T(8,128)(2,1)}, u32[]{:S(2)}, u32[]{:S(2)}) async-start(bf16[4,1536,192]{1,2,0:T(8,128)(2,1)} %broadcast_in_dim.20), calls=%async_computation | async-start | bytes 4718592 | tf_op jit(solution)/shard_map/all_to_all | solution.py:42
  183.3 52.0 %copy-start.2 = (f32[16,8,6]{0,1,2:T(8,128)S(1)}, f32[16,8,6]{0,1,2:T(8,128)}, u32[]{:S(2)}) copy-start(f32[16,8,6]{0,1,2:T(8,128)} %copy.417) | copy-start | bytes 9220
  183.3 52.0 %copy-start.3 = (f32[16,8,6]{0,1,2:T(8,128)S(1)}, f32[16,8,6]{0,1,2:T(8,128)}, u32[]{:S(2)}) copy-start(f32[16,8,6]{0,1,2:T(8,128)} %copy.415) | copy-start | bytes 9220
  310.3 3.5 copy-start.4
  310.3 3.5 copy-start.5
  310.3 3.5 copy-start.6
  310.3 3.5 copy-start.7
  313.8 10.0 %copy-start.9 = (f32[16,8,128]{2,1,0:T(8,128)S(1)}, f32[16,8,128]{2,1,0:T(8,128)}, u32[]{:S(2)}) copy-start(f32[16,8,128]{2,1,0:T(8,128)} %copy.375) | copy-start | bytes 196612
  313.8 10.0 %copy-start.10 = (f32[16,8,6]{1,2,0:T(8,128)S(1)}, f32[16,8,6]{1,2,0:T(8,128)}, u32[]{:S(2)}) copy-start(f32[16,8,6]{1,2,0:T(8,128)} %copy.372) | copy-start | bytes 9220
  313.8 10.0 %copy-start.11 = (f32[16,8,6]{1,2,0:T(8,128)S(1)}, f32[16,8,6]{1,2,0:T(8,128)}, u32[]{:S(2)}) copy-start(f32[16,8,6]{1,2,0:T(8,128)} %copy.373) | copy-start | bytes 9220
  313.8 10.0 %copy-start.12 = (f32[16,8,6]{1,2,0:T(8,128)S(1)}, f32[16,8,6]{1,2,0:T(8,128)}, u32[]{:S(2)}) copy-start(f32[16,8,6]{1,2,0:T(8,128)} %copy.374) | copy-start | bytes 9220
  313.8 10.0 %copy-start.13 = (f32[16,8,6]{1,2,0:T(8,128)S(1)}, f32[16,8,6]{1,2,0:T(8,128)}, u32[]{:S(2)}) copy-start(f32[16,8,6]{1,2,0:T(8,128)} %copy.394) | copy-start | bytes 9220
  321.2 4.1 copy-start.14
  321.2 14.0 %copy-start.18 = (bf16[192]{0:T(256)(128)(2,1)S(1)}, bf16[192]{0:T(256)(128)(2,1)}, u32[]{:S(2)}) copy-start(bf16[192]{0:T(256)(128)(2,1)} %param.22) | copy-start | bytes 1156
  321.2 25.7 %copy-start.17 = (bf16[192,4]{0,1:T(4,128)(2,1)S(1)}, bf16[192,4]{0,1:T(4,128)(2,1)}, u32[]{:S(2)}) copy-start(bf16[192,4]{0,1:T(4,128)(2,1)} %param.23) | copy-start | bytes 4612
  321.2 31.1 %copy-start.15 = (s32[16,2]{0,1:T(2,128)S(1)}, s32[16,2]{0,1:T(2,128)}, u32[]{:S(2)}) copy-start(s32[16,2]{0,1:T(2,128)} %param.24) | copy-start | bytes 388
  328.6 18.3 %all-to-all-start.1 = ((f32[32,1,16]{2,1,0:T(1,128)}), f32[32,1,16]{2,1,0:T(1,128)S(1)}, u32[]{:S(2)}, u32[]{:S(2)}) async-start(f32[32,1,16]{2,1,0:T(1,128)} %broadcast_in_dim.21), calls=%async_computation.1 | async-start | bytes 32768 | tf_op jit(solution)/shard_map/all_to_all | solution.py:42
  347.7 18.0 %all-to-all-start.2 = ((f32[32,16,4]{1,2,0:T(4,128)}), f32[32,16,4]{1,2,0:T(4,128)S(1)}, u32[]{:S(2)}, u32[]{:S(2)}) async-start(f32[32,16,4]{1,2,0:T(4,128)} %broadcast_in_dim.22), calls=%async_computation.2 | async-start | bytes 131072 | tf_op jit(solution)/shard_map/all_to_all | solution.py:42
  367.1 9.3 %all-to-all-start.3 = ((bf16[4,12,192]{2,1,0:T(8,128)(2,1)}), bf16[4,12,192]{2,1,0:T(8,128)(2,1)S(1)}, u32[]{:S(2)}, u32[]{:S(2)}) async-start(bf16[4,12,192]{2,1,0:T(8,128)(2,1)} %convolution_convert_fusion), calls=%async_computation.3 | async-start | bytes 65536 | tf_op jit(solution)/shard_map/all_to_all | solution.py:177
Sparse Core Ops, SparseCore 0:
  99.3 86.8 all-gather.6
where the time goes:
time: 529 us; the launch traced here: 522 us
  blocking collectives  289 us (55%)
  local copies, waits for them, and re-layouts  131 us (25%)
  other arithmetic  26.3 us (5%)
  waiting for transfers between devices  25 us (5%)
  starting transfers between devices  20.5 us (4%)
  matrix products  17.6 us (3%)
  between operations  13.8 us (3%)
    all_gather x5, blocking collectives, combined_by_axis(): pieces = jax.tree.map(lambda part: lax.all_gather(part, axis), value)  84.4 us
    all_to_all x1, blocking collectives, summed_on_arrival(): parts = lax.all_to_all(in_blocks(value, dim, count), axis, 0, 0, tiled=True)  83.6 us
    unnamed x78, local copies, waits for them, and re-layouts  61.3 us
    all_gather x1, blocking collectives, on_device(): lax.all_gather(query, TP, axis=1, tiled=True)  51.5 us
    all_gather x2, blocking collectives, all_blocks(): parts = lax.all_gather(parts, axes[k])  33.2 us
    all_gather x1, blocking collectives, side_by_side(): lax.all_gather(both, axis, axis=dim, tiled=True)  27.9 us
    all_to_all x3, waiting for transfers between devices, sent_to_all(): lax.all_to_all(jnp.broadcast_to(value[None], (count, *value.shape)), axis...  25 us
    exp x16, local copies, waits for them, and re-layouts, join_softmax(): first_scale = jnp.exp(first[0] - joined)  22.7 us
  transfers between devices with their start and end apart: 5, of which 2 were waited for; matrix products, arithmetic and copies ran while one was open for 25% of the time, Pallas kernels for 0%

commit v1 on v0

v1 whole, which is shorter than its diff:
```python
import functools

import jax
import jax.numpy as jnp
from jax import lax
from jax.experimental import pallas as pl
from jax.experimental.pallas import tpu as pltpu
from jax.sharding import PartitionSpec as P

HD = 128
F32 = jnp.float32
BF16 = jnp.bfloat16
MESH = pl.DeviceIdType.MESH
FLOOR = -1e30


def lanes(shape):
    return lax.broadcasted_iota(jnp.int32, shape, len(shape) - 1)


def pick(flag, first, second):
    return jnp.where(jnp.full(first.shape, flag, jnp.int32) == 0, first, second)


def joined(a0, a1, b0, b1):
    lane = lanes(a0.shape)
    r0, r1 = pltpu.roll(b0, 64, 1), pltpu.roll(b1, 64, 1)
    return a0, jnp.where(lane < 64, a1, r0), jnp.where(lane < 64, r0, r1)


def layer(
    Z, X, D, P_LOC,
    pk, gr, lens, routes, kc, vc, wo, gw, uw, dw,
    out,
    ppk, pgr, kbuf, vbuf, wbuf, gbuf, ubuf, dbuf,
    kvt, kvo, qbuf, obuf, rbuf, abuf, axb, pbuf, prs, prb,
    hbuf, tbuf, irb, inner, ysend, yrecv, ymine, xsend, xrecv, acc, zsend, zrecv, fsend, frecv,
    lsem, dss, dsr, qs, qr, kvs, kvr, os_, or_, as_, ar, axs, axr, prss, prsr,
    hs, hr, ts, tr, hxs, hxr, hds, hdr, ixs, ixr, ids, idr, ys, yr, xs, xr, zs, zr, fs, fr,
):
    t = lax.axis_index("tp")
    s = lax.axis_index("sub")
    c = t % 2
    z = t // 2
    o = 1 - c
    partner = t + 1 - 2 * c
    CW = 3 * HD
    KVH = Z // 2
    DX = D // X
    scale = 1.0 / HD**0.5

    def remote(src, dst, ssem, rsem, **where):
        return pltpu.make_async_remote_copy(
            src_ref=src, dst_ref=dst, send_sem=ssem, recv_sem=rsem,
            device_id=where, device_id_type=MESH,
        )

    def over_z(fn):
        def step(k, carry):
            d = Z // 2 + jnp.where(k % 2 == 0, k // 2, -((k + 1) // 2))
            fn(d)
            return carry

        lax.fori_loop(0, Z - 1, step, 0)

    def chip(i, width):
        return pl.ds(pl.multiple_of(i * width, 128), width)

    half = pl.ds(pl.multiple_of(8 * c, 8), 8)
    other = pl.ds(pl.multiple_of(8 * o, 8), 8)
    local = [
        pltpu.make_async_copy(kc.at[half], kbuf.at[c], lsem.at[0]),
        pltpu.make_async_copy(vc.at[half], vbuf.at[c], lsem.at[1]),
        pltpu.make_async_copy(wo, wbuf.at[c], lsem.at[2]),
        pltpu.make_async_copy(gw.at[0], gbuf, lsem.at[3]),
        pltpu.make_async_copy(uw.at[0], ubuf, lsem.at[4]),
        pltpu.make_async_copy(dw.at[0], dbuf, lsem.at[5]),
    ]
    for copy in local:
        copy.start()

    barrier = pltpu.get_barrier_semaphore()

    def greet(d):
        pl.semaphore_signal(
            barrier, inc=1, device_id={"tp": 2 * ((z + d) % Z) + c}, device_id_type=MESH
        )

    over_z(greet)
    for d in range(1, X):
        pl.semaphore_signal(barrier, inc=1, device_id={"sub": (s + d) % X}, device_id_type=MESH)
    pl.semaphore_signal(barrier, inc=1, device_id={"tp": partner}, device_id_type=MESH)
    pl.semaphore_wait(barrier, Z - 1 + X - 1 + 1)

    swaps = [
        remote(pk.at[o], ppk, dss.at[0], dsr.at[0], tp=partner),
        remote(gr, pgr, dss.at[1], dsr.at[1], tp=partner),
        remote(kc.at[other], kbuf.at[c], dss.at[2], dsr.at[2], tp=partner),
        remote(vc.at[other], vbuf.at[c], dss.at[3], dsr.at[3], tp=partner),
        remote(wo, wbuf.at[c], dss.at[4], dsr.at[4], tp=partner),
    ]
    for copy in swaps:
        copy.start()
    swaps[0].wait_recv()

    mine = pk[c].astype(F32)
    theirs = ppk[...].astype(F32)
    first, second = pick(c, mine, theirs), pick(c, theirs, mine)
    lane = lanes((8, HD))

    def tile(value, k):
        return value[:, HD * k : HD * (k + 1)]

    q_own = joined(tile(first, 0), tile(first, 1), tile(second, 0), tile(second, 1))
    hid = joined(tile(first, 2), tile(first, 3), tile(second, 2), tile(second, 3))
    qbuf[:, chip(z, CW)] = jnp.concatenate(q_own, axis=1).astype(BF16)

    def send_q(d):
        to = (z + d) % Z
        remote(
            qbuf.at[:, chip(z, CW)], qbuf.at[:, chip(z, CW)], qs.at[to], qr.at[z], tp=2 * to + c
        ).start()

    over_z(send_q)
    kvt[...] = jnp.where(lane < 64, pltpu.roll(tile(first, 1), 64, 1), tile(second, 1)).astype(BF16)
    z_pair = z + 1 - 2 * (z % 2)
    kv_copy = remote(kvt, kvo, kvs.at[0], kvr.at[0], tp=2 * z_pair + c)
    kv_copy.start()

    local[0].wait()
    local[1].wait()
    swaps[2].wait_recv()
    swaps[3].wait_recv()

    def wait_q(d):
        at = (z + d) % Z
        remote(
            qbuf.at[:, chip(at, CW)], qbuf.at[:, chip(at, CW)], qs.at[at], qr.at[at], tp=2 * at + c
        ).wait_recv()

    over_z(wait_q)

    cols = 2 * 8 * P_LOC
    group = 6
    rows = group * 8
    col = lax.broadcasted_iota(jnp.int32, (rows, cols), 1)
    row = lax.broadcasted_iota(jnp.int32, (rows, cols), 0)
    position = (2 * z + col // (8 * P_LOC)) * P_LOC + col % P_LOC
    length = jnp.concatenate([jnp.broadcast_to(lens[half, :], (8, cols))] * group, axis=0)
    valid = (row % 8 == (col % (8 * P_LOC)) // P_LOC) & (position < length)
    for g in range(KVH):
        at = slice(HD * g, HD * (g + 1))
        q_g = qbuf[:, group * HD * g : group * HD * (g + 1)].astype(F32)
        q_g = jnp.concatenate([tile(q_g, i) for i in range(group)], axis=0).astype(BF16)
        keys = kbuf[:, :, :, at].reshape(cols, HD)
        values = vbuf[:, :, :, at].reshape(cols, HD)
        scores = (
            lax.dot_general(q_g, keys, (((1,), (1,)), ((), ())), preferred_element_type=F32) * scale
        )
        scores = jnp.where(valid, scores, FLOOR)
        top = jnp.max(scores, axis=1, keepdims=True).astype(BF16).astype(F32)
        weights = jnp.where(valid, jnp.exp(scores - top), 0.0)
        total = jnp.sum(weights, axis=1, keepdims=True)
        summed = jnp.dot(weights.astype(BF16), values, preferred_element_type=F32)
        high = total.astype(BF16).astype(F32)
        low = total - high
        for k in range(2):
            stats = jnp.zeros((8, HD), F32)
            parts = []
            for j in range(3):
                at_row = slice(8 * (3 * k + j), 8 * (3 * k + j + 1))
                parts.append(summed[at_row])
                stats = jnp.where(lane == j, top[at_row], stats)
                stats = jnp.where(lane == 32 + j, high[at_row], stats)
                stats = jnp.where(lane == 64 + j, low[at_row], stats)
            block = jnp.concatenate(parts + [stats], axis=1).astype(BF16)
            obuf[:, 4 * HD * (2 * g + k) : 4 * HD * (2 * g + k + 1)] = block

    def send_o(d):
        to = (z + d) % Z
        remote(
            obuf.at[:, chip(to, 4 * HD)], rbuf.at[z], os_.at[to], or_.at[z], tp=2 * to + c
        ).start()

    over_z(send_o)
    rbuf[z] = obuf[:, chip(z, 4 * HD)]
    kv_copy.wait_recv()
    t_mine, t_pair = kvt[...].astype(F32), kvo[...].astype(F32)
    even, odd = pick(z % 2, t_mine, t_pair), pick(z % 2, t_pair, t_mine)

    def quarters(shifts):
        w = [pltpu.roll(v, k, 1) if k else v for v, k in zip((even, even, odd, odd), shifts)]
        low_half = jnp.where(lane < 32, w[0], w[1])
        high_half = jnp.where(lane < 96, w[2], w[3])
        return jnp.where(lane < 64, low_half, high_half)

    key_own = quarters((0, 96, 64, 32))
    value_own = quarters((96, 64, 32, 0))
    own = jnp.zeros((8, HD), F32)
    for j in range(3):
        dot = jnp.sum(q_own[j] * key_own, axis=1, keepdims=True) * scale
        own = jnp.where(lane == j, dot, own)

    def wait_o(d):
        at = (z + d) % Z
        remote(
            obuf.at[:, chip(at, 4 * HD)], rbuf.at[at], os_.at[at], or_.at[at], tp=2 * at + c
        ).wait_recv()

    over_z(wait_o)
    tops = [rbuf[k, :, 3 * HD :].astype(F32) for k in range(Z)]
    top = own
    for part in tops:
        top = jnp.maximum(top, part)
    own_weight = jnp.where(lane < 3, jnp.exp(own - top), 0.0)
    total = own_weight
    factors = []
    for part in tops:
        factor = jnp.where(lane < 3, jnp.exp(part - top), 0.0)
        factors.append(factor)
        total = total + factor * (pltpu.roll(part, 96, 1) + pltpu.roll(part, 64, 1))
    inverse = jnp.where(lane < 3, 1.0 / jnp.where(lane < 3, total, 1.0), 0.0)
    own_weight = own_weight * inverse
    parts = []
    for j in range(3):
        value = own_weight[:, j : j + 1] * value_own
        for k in range(Z):
            factor = factors[k] * inverse
            value = value + factor[:, j : j + 1] * rbuf[k, :, HD * j : HD * (j + 1)].astype(F32)
        parts.append(value)
    abuf[:, chip(z, CW)] = jnp.concatenate(parts, axis=1).astype(BF16)

    def send_a(d):
        to = (z + d) % Z
        remote(
            abuf.at[:, chip(z, CW)], abuf.at[:, chip(z, CW)], as_.at[to], ar.at[z], tp=2 * to + c
        ).start()

    over_z(send_a)
    local[2].wait()
    swaps[1].wait_recv()
    swaps[4].wait_recv()

    def wait_a(d):
        at = (z + d) % Z
        remote(
            abuf.at[:, chip(at, CW)], abuf.at[:, chip(at, CW)], as_.at[at], ar.at[at], tp=2 * at + c
        ).wait_recv()

    over_z(wait_a)

    def x_copy(d, src, dst, ssem, rsem, frm=False):
        to = (s + d) % X
        return remote(src(to), dst(to if frm else s), ssem.at[to], rsem.at[to if frm else s], sub=to)

    def attn_copy(d, frm=False):
        return x_copy(
            d, lambda to: abuf.at[:, chip(to, DX)], lambda at: axb.at[at], axs, axr, frm
        )

    for d in range(1, X):
        attn_copy(d).start()
    axb[s] = abuf[:, chip(s, DX)]
    for d in range(1, X):
        attn_copy(d, True).wait_recv()
    left = axb[...].astype(F32).reshape(8 * X, DX).astype(BF16)
    for k in range(2):
        pbuf[k, :, HD:] = jnp.zeros((8 * X, HD), F32)
        pbuf[k, :, : D // (2 * Z)] = jnp.dot(left, wbuf[k], preferred_element_type=F32)
    both = [pbuf[k] for k in range(2)]
    tiles = joined(tile(both[0], 0), tile(both[0], 1), tile(both[1], 0), tile(both[1], 1))
    prs[...] = jnp.concatenate(tiles, axis=1).reshape(X, 8, CW)

    def proj_copy(d, frm=False):
        return x_copy(d, lambda to: prs.at[to], lambda at: prb.at[at], prss, prsr, frm)

    for d in range(1, X):
        proj_copy(d).start()
    resid = jnp.concatenate(hid, axis=1) + prs[s]
    g_mine, g_theirs = gr[...], pgr[...]
    ga, gb = pick(c, g_mine, g_theirs), pick(c, g_theirs, g_mine)
    gains = jnp.concatenate(joined(tile(ga, 0), tile(ga, 1), tile(gb, 0), tile(gb, 1)), axis=1)
    for d in range(1, X):
        proj_copy(d, True).wait_recv()
        resid = resid + prb[(s + d) % X]
    gained = resid * gains[0:1]
    hbuf[c, s, :, chip(z, CW)] = gained.astype(BF16)
    stats = jnp.where(lane == 0, jnp.sum(resid * resid, axis=1, keepdims=True), 0.0)
    for e in range(X):
        logit = jnp.sum(gained * gains[e + 1 : e + 2], axis=1, keepdims=True)
        stats = jnp.where(lane == e + 1, logit, stats)
    tbuf[z] = stats

    def h_copy(d):
        to = (z + d) % Z
        return remote(
            hbuf.at[c, s, :, chip(z, CW)], hbuf.at[c, s, :, chip(z, CW)],
            hs.at[to], hr.at[z], tp=2 * to + c,
        )

    def t_copy(d):
        to = (z + d) % Z
        return remote(tbuf.at[z], tbuf.at[z], ts.at[to], tr.at[z], tp=2 * to + c)

    over_z(lambda d: t_copy(d).start())
    over_z(lambda d: h_copy(d).start())

    def wait_t(d):
        at = (z + d) % Z
        remote(tbuf.at[at], tbuf.at[at], ts.at[at], tr.at[at], tp=2 * at + c).wait_recv()

    over_z(wait_t)
    sums = tbuf[0]
    for k in range(1, Z):
        sums = sums + tbuf[k]
    inv_root = 1.0 / jnp.sqrt(sums[:, 0:1] / D + 1e-05)
    irb[c, s] = jnp.broadcast_to(inv_root, (8, HD))

    def h_x(d, frm=False):
        at = (s + d) % X
        src = at if frm else s
        return (
            remote(hbuf.at[c, src], hbuf.at[c, src], hxs.at[at], hxr.at[src], sub=at),
            remote(irb.at[c, src], irb.at[c, src], ixs.at[at], ixr.at[src], sub=at),
        )

    def h_d(src, core):
        return (
            remote(hbuf.at[core, src], hbuf.at[core, src], hds.at[src], hdr.at[src], tp=partner),
            remote(irb.at[core, src], irb.at[core, src], ids.at[src], idr.at[src], tp=partner),
        )

    for d in range(1, X):
        h_x(d)[1].start()
    h_d(s, c)[1].start()
    logits = sums * inv_root
    picked = routes[half, :]
    hot_first, hot_second = lane == picked[:, 0:1] + 1, lane == picked[:, 1:2] + 1
    l_first = jnp.sum(jnp.where(hot_first, logits, 0.0), axis=1, keepdims=True)
    l_second = jnp.sum(jnp.where(hot_second, logits, 0.0), axis=1, keepdims=True)
    w_first = 1.0 / (1.0 + jnp.exp(l_second - l_first))
    w_second = 1.0 / (1.0 + jnp.exp(l_first - l_second))
    dense = jnp.where(hot_first, w_first, 0.0) + jnp.where(hot_second, w_second, 0.0)

    def share(e):
        return jnp.sum(jnp.where(lane == e + 1, dense, 0.0), axis=1, keepdims=True)

    def wait_h(d):
        at = (z + d) % Z
        remote(
            hbuf.at[c, s, :, chip(at, CW)], hbuf.at[c, s, :, chip(at, CW)],
            hs.at[at], hr.at[at], tp=2 * at + c,
        ).wait_recv()

    over_z(wait_h)
    for d in range(1, X):
        h_x(d)[0].start()
    h_d(s, c)[0].start()
    for d in range(1, X):
        for k in (1, 0):
            h_x(d, True)[k].wait_recv()
            h_d((s + d) % X, c)[k].start()
    for d in range(X):
        for k in (1, 0):
            h_d((s + d) % X, o)[k].wait_recv()
    for copy in local[3:]:
        copy.wait()

    N = 16 * X
    F = gbuf.shape[1]
    step = 6 * HD
    gate = jnp.zeros((N, F), F32)
    up = jnp.zeros((N, F), F32)
    for k in range(0, D, step):
        left = hbuf[:, :, :, k : k + step].astype(F32).reshape(N, step).astype(BF16)
        gate = gate + jnp.dot(left, gbuf[k : k + step], preferred_element_type=F32)
        up = up + jnp.dot(left, ubuf[k : k + step], preferred_element_type=F32)
    inv = irb[...].reshape(N, HD)
    inv = jnp.concatenate([inv] * (F // HD), axis=1)
    gate, up = gate * inv, up * inv
    inner[...] = (gate / (1.0 + jnp.exp(-gate)) * up).reshape(2, N // 2, F).astype(BF16)
    left = inner[o]
    for k in range(0, D, step):
        part = jnp.dot(left, dbuf[:, k : k + step], preferred_element_type=F32)
        ysend[:, :, k : k + step] = part.reshape(X, 8, step).astype(BF16)
    y_copy = remote(ysend, yrecv, ys.at[0], yr.at[0], tp=partner)
    y_copy.start()
    left = inner[c]
    for k in range(0, D, step):
        part = jnp.dot(left, dbuf[:, k : k + step], preferred_element_type=F32)
        ymine[:, :, k : k + step] = part.reshape(X, 8, step)
    y_copy.wait_recv()

    def y_x(d, frm=False):
        return x_copy(d, lambda to: xsend.at[to], lambda at: xrecv.at[at], xs, xr, frm)

    for d in range(1, X):
        to = (s + d) % X
        xsend[to] = (ymine[to] + yrecv[to].astype(F32)).astype(BF16)
        y_x(d).start()
    acc[...] = share(s) * (ymine[s] + yrecv[s].astype(F32))
    for d in range(1, X):
        y_x(d, True).wait_recv()
        at = (s + d) % X
        acc[...] += share(at) * xrecv[at].astype(F32)
    zsend[...] = acc[...].astype(BF16)

    def send_z(d):
        to = (z + d) % Z
        remote(
            zsend.at[:, chip(to, CW)], zrecv.at[z], zs.at[to], zr.at[z], tp=2 * to + c
        ).start()

    over_z(send_z)
    zrecv[z] = jnp.zeros((8, CW), BF16)
    result = resid + acc[:, chip(z, CW)]

    def wait_z(d):
        at = (z + d) % Z
        remote(
            zsend.at[:, chip(at, CW)], zrecv.at[at], zs.at[at], zr.at[at], tp=2 * at + c
        ).wait_recv()

    over_z(wait_z)
    for k in range(Z):
        result = result + zrecv[k].astype(F32)

    r1, r2 = pltpu.roll(tile(result, 1), 64, 1), pltpu.roll(tile(result, 2), 64, 1)
    v_first = result[:, : 2 * HD]
    v_second = jnp.concatenate([jnp.where(lane < 64, r1, r2), r2], axis=1)
    fsend[...] = pick(c, v_second, v_first).astype(BF16)
    f_copy = remote(fsend, frecv, fs.at[0], fr.at[0], tp=partner)
    f_copy.start()
    kept = pick(c, v_first, v_second)

    def sent(d):
        to = (z + d) % Z
        for src, ssem in (
            (qbuf.at[:, chip(z, CW)], qs), (obuf.at[:, chip(to, 4 * HD)], os_),
            (abuf.at[:, chip(z, CW)], as_), (hbuf.at[c, s, :, chip(z, CW)], hs),
            (tbuf.at[z], ts), (zsend.at[:, chip(to, CW)], zs),
        ):
            remote(src, src, ssem.at[to], qr.at[z], tp=2 * to + c).wait_send()

    over_z(sent)
    for copy in swaps:
        copy.wait_send()
    kv_copy.wait_send()
    y_copy.wait_send()
    for d in range(1, X):
        attn_copy(d).wait_send()
        proj_copy(d).wait_send()
        y_x(d).wait_send()
        for copy in h_x(d):
            copy.wait_send()
    for d in range(X):
        for copy in h_d((s + d) % X, c):
            copy.wait_send()
    f_copy.wait()
    came = frecv[...].astype(F32)
    whole = jnp.concatenate([pick(c, kept, came), pick(c, came, kept)], axis=0)
    out[...] = whole[:, : D // (2 * Z)].astype(BF16)


def on_device(
    Z, X,
    hidden_in, query, key_new, value_new, key_cache, value_cache, lengths,
    out_weight, norm_gain, router_weight, routes, gate_weight, up_weight, down_weight,
):
    width = hidden_in.shape[1]
    D = width * 2 * Z
    P_LOC = key_cache.shape[1]
    F = gate_weight.shape[2]
    CW = 3 * HD
    pk = jnp.concatenate([query, key_new, value_new, hidden_in], axis=1)
    pk = jnp.pad(pk, ((0, 0), (0, 4 * HD - pk.shape[1]))).reshape(2, 8, 4 * HD)
    gr = jnp.concatenate([norm_gain[None].astype(F32), router_weight.astype(F32).T], axis=0)
    gr = jnp.pad(gr, ((0, 8 - gr.shape[0]), (0, 2 * HD - width)))
    vm = pl.BlockSpec(memory_space=pltpu.VMEM)
    anywhere = pl.BlockSpec(memory_space=pl.ANY)
    dma = pltpu.SemaphoreType.DMA
    V = pltpu.VMEM
    scratch = [
        V((8, 4 * HD), BF16), V((8, 2 * HD), F32),
        V((2, 8, P_LOC, key_cache.shape[2]), BF16), V((2, 8, P_LOC, key_cache.shape[2]), BF16),
        V((2, *out_weight.shape), BF16),
        V((D, F), BF16), V((D, F), BF16), V((F, D), BF16),
        V((8, HD), BF16), V((8, HD), BF16),
        V((8, D), BF16),
        V((8, Z * 4 * HD), BF16), V((Z, 8, 4 * HD), BF16),
        V((8, D), BF16), V((X, 8, D // X), BF16),
        V((2, 8 * X, 2 * HD), F32), V((X, 8, CW), F32), V((X, 8, CW), F32),
        V((2, X, 8, D), BF16), V((Z, 8, HD), F32), V((2, X, 8, HD), F32),
        V((2, 8 * X, F), BF16),
        V((X, 8, D), BF16), V((X, 8, D), BF16), V((X, 8, D), F32),
        V((X, 8, D), BF16), V((X, 8, D), BF16),
        V((8, D), F32), V((8, D), BF16), V((Z, 8, CW), BF16),
        V((8, 2 * HD), BF16), V((8, 2 * HD), BF16),
        dma((6,)), dma((5,)), dma((5,)),
        dma((Z,)), dma((Z,)), dma((1,)), dma((1,)),
        dma((Z,)), dma((Z,)), dma((Z,)), dma((Z,)),
        dma((X,)), dma((X,)), dma((X,)), dma((X,)),
        dma((Z,)), dma((Z,)), dma((Z,)), dma((Z,)),
        dma((X,)), dma((X,)), dma((X,)), dma((X,)), dma((X,)), dma((X,)), dma((X,)), dma((X,)),
        dma((1,)), dma((1,)), dma((X,)), dma((X,)), dma((Z,)), dma((Z,)), dma((1,)), dma((1,)),
    ]
    return pl.pallas_call(
        functools.partial(layer, Z, X, D, P_LOC),
        out_shape=jax.ShapeDtypeStruct(hidden_in.shape, BF16),
        in_specs=[vm] * 4 + [anywhere] * 6,
        out_specs=vm,
        scratch_shapes=scratch,
        compiler_params=pltpu.CompilerParams(
            collective_id=0, has_side_effects=True, vmem_limit_bytes=56 * 1024 * 1024
        ),
        name="decode_layer",
    )(
        pk, gr, lengths[:, None], routes, key_cache, value_cache, out_weight,
        gate_weight, up_weight, down_weight,
    )


def solution(mesh):
    Z, X = mesh.shape["tp"] // 2, mesh.shape["sub"]
    rows = P(("rep", "sub"), "tp")
    return jax.shard_map(
        functools.partial(on_device, Z, X),
        mesh=mesh,
        in_specs=(
            rows, rows, rows, rows,
            P(("rep", "sub"), "tp", None), P(("rep", "sub"), "tp", None), P(("rep", "sub")),
            P("sub", "tp"), P("tp"), P("tp", None), P(("rep", "sub"), None),
            P("sub", None, "tp"), P("sub", None, "tp"), P("sub", "tp", None),
        ),
        out_specs=rows,
        check_vma=False,
    )
```

time: 529 us -> 112 us (0.21); the launches traced: 522 us -> 112 us
  blocking collectives: 289 us -> 0 us
  local copies, waits for them, and re-layouts: 131 us -> 6.84 us
  Pallas kernels: 0 us -> 102 us
  waiting for transfers between devices: 25 us -> 0 us
  other arithmetic: 26.3 us -> 2.71 us
  starting transfers between devices: 20.5 us -> 0 us
  matrix products: 17.6 us -> 0 us
  between operations: 13.8 us -> 0.01 us
    all_gather x9 -> x0, blocking collectives: 197 us -> none  [the longest x5 84.4 us: combined_by_axis(): pieces = jax.tree.map(lambda part: lax.all_gather(part, axis), value)]
    pallas_call x0 -> x1, Pallas kernels: none -> 102 us  [on_device(): pl.pallas_call(functools.partial(layer, Z, X, D, P_LOC), out_shape=jax.Sh...]
    all_to_all x2 -> x0, blocking collectives: 91.6 us -> none  [the longest x1 83.6 us: summed_on_arrival(): parts = lax.all_to_all(in_blocks(value, dim, count), axis, 0, 0, tiled=True)]
    unnamed x78 -> x3, local copies, waits for them, and re-layouts: 61.3 us -> 4.86 us
    exp x33 -> x0, local copies, waits for them, and re-layouts: 46.3 us -> none  [the longest x16 22.7 us: join_softmax(): first_scale = jnp.exp(first[0] - joined)]
    all_to_all x4 -> x0, waiting for transfers between devices: 25 us -> none  [the longest x3 25 us: sent_to_all(): lax.all_to_all(jnp.broadcast_to(value[None], (count, *value.shape)), axis...]
    all_to_all x4 -> x0, starting transfers between devices: 20.5 us -> none  [the longest x3 15.9 us: sent_to_all(): lax.all_to_all(jnp.broadcast_to(value[None], (count, *value.shape)), axis...]
    dot_general x9 -> x0, matrix products: 17.6 us -> none  [the longest x1 5.55 us: on_device(): result = jnp.dot(inner, down_local, preferred_element_type=jnp.float32)]
  transfers between devices with their start and end apart: 5 -> 0, of which waited for: 2 -> 0; matrix products, arithmetic and copies ran while one was open for 25% -> 0% of each run, Pallas kernels for 0% -> 0%
where the time goes in v1:
time: 112 us
  Pallas kernels  102 us (91%)
  local copies, waits for them, and re-layouts  6.84 us (6%)
  other arithmetic  2.71 us (2%)
    pallas_call x1, Pallas kernels, on_device(): pl.pallas_call(functools.partial(layer, Z, X, D, P_LOC), out_shape=jax.Sh...  102 us
    unnamed x3, local copies, waits for them, and re-layouts  4.86 us

profile of v1, /device:TPU:33, one launch (start us, length us, event | category | flops | bytes accessed | tf_op | source)
XLA Modules:
  0.0 111.7 jit_solution(5393925926044503208)
XLA Ops:
  0.0 0.7 convert_element_type.9
  0.7 1.3 %fusion.14.gr = f32[8,256]{1,0:T(8,128)} fusion(bf16[4,192]{1,0:T(4,128)(2,1)} %bitcast.4, bf16[1,192]{1,0:T(2,128)(2,1)S(1)} %convert_element_type.9), kind=kLoop, calls=%fused_computation.17 | loop fusion | flops 22528 | bytes 10112 | tf_op jit(solution)/shard_map/jit(_pad)/pad | solution.py:478
  1.9 1.3 %copy.15.lens = s32[16,1]{1,0:T(8,128)} copy(s32[16,1]{0,1:T(1,128)} %bitcast.5) | data formatting | bytes 128 | tf_op jit(solution)/shard_map/broadcast_in_dim | solution.py:518
  3.3 1.3 %copy.16.routes = s32[16,2]{1,0:T(8,128)} copy(s32[16,2]{0,1:T(2,128)} %param.24) | data formatting | bytes 256 | tf_op args[10]
  4.6 1.4 %fusion.7.pk = bf16[2,8,512]{2,1,0:T(8,128)(2,1)} fusion(bf16[16,192]{1,0:T(8,128)(2,1)} %param.14, bf16[16,32]{1,0:T(8,128)(2,1)} %param.17, bf16[16,32]{1,0:T(8,128)(2,1)} %param.16, bf16[16,192]{1,0:T(8,128)(2,1)} %param.15), kind=kLoop, calls=%fused_computation.8 | loop fusion | flops 106496 | bytes 30720 | tf_op jit(solution)/shard_map/reshape | solution.py:476
  6.0 2.2 %copy.17.wo = bf16[1536,192]{1,0:T(8,128)(2,1)} copy(bf16[1536,192]{0,1:T(8,128)(2,1)} %param.21) | data formatting | bytes 1179648 | tf_op args[7]
  8.3 102.1 %decode_layer.1 = bf16[16,192]{1,0:T(8,128)(2,1)} custom-call(bf16[2,8,512]{2,1,0:T(8,128)(2,1)} %fusion.7.pk, f32[8,256]{1,0:T(8,128)} %fusion.14.gr, s32[16,1]{1,0:T(8,128)} %copy.15.lens, s32[16,2]{1,0:T(8,128)} %copy.16.routes, bf16[16,32,1024]{2,1,0:T(8,128)(2,1)} %kc.1, bf16[16,32,1024]{2,1,0:T(8,128)(2,1)} %vc.1, bf16[1536,192]{1,0:T(8,128)(2,1)} %copy.17.wo, ...), custom_call_target="tpu_custom_call" | custom-call | tf_op jit(solution)/shard_map/decode_layer/pallas_call | solution.py:507
  110.4 1.3 %copy.19 = bf16[16,192]{1,0:T(8,128)(2,1)} copy(bf16[16,192]{1,0:T(8,128)(2,1)} %decode_layer.1) | data formatting | bytes 12288

commit v2 on v1

v2 whole, which is shorter than its diff:
```python
import functools

import jax
import jax.numpy as jnp
from jax import lax
from jax.experimental import pallas as pl
from jax.experimental.pallas import tpu as pltpu
from jax.sharding import PartitionSpec as P

HD = 128
F32 = jnp.float32
BF16 = jnp.bfloat16
MESH = pl.DeviceIdType.MESH
FLOOR = -1e30
CHUNKS = 4
SEMAPHORES = 96


def lanes(shape):
    return lax.broadcasted_iota(jnp.int32, shape, len(shape) - 1)


def pick(flag, first, second):
    return jnp.where(jnp.full(first.shape, flag, jnp.int32) == 0, first, second)


def joined(a0, a1, b0, b1):
    lane = lanes(a0.shape)
    r0, r1 = pltpu.roll(b0, 64, 1), pltpu.roll(b1, 64, 1)
    return a0, jnp.where(lane < 64, a1, r0), jnp.where(lane < 64, r0, r1)


def layer(
    Z, X, D, P_LOC,
    hidden, query, k_new, v_new, lens, routes, gain, router, kc, vc, wo, gw, uw, dw,
    out,
    phid, pq, pk, pv, pgain, prouter, small,
    kbuf, vbuf, wbuf, gbuf, ubuf, dbuf,
    kvt, kvo, qbuf, obuf, rbuf, abuf, pbuf,
    hbuf, tbuf, irb, inner, ysend, yrecv, ymine, xsend, xrecv, acc, zsend, zrecv, fsend, frecv,
    lsem, sems,
):
    t = lax.axis_index("tp")
    s = lax.axis_index("sub")
    c = t % 2
    z = t // 2
    o = 1 - c
    partner = t + 1 - 2 * c
    CW = 3 * HD
    KVH = Z // 2
    DX = D // X
    taken = iter(range(SEMAPHORES))
    scale = 1.0 / HD**0.5

    def sem():
        return sems.at[next(taken)]

    def remote(src, dst, ssem, rsem, **where):
        return pltpu.make_async_remote_copy(
            src_ref=src, dst_ref=dst, send_sem=ssem, recv_sem=rsem,
            device_id=where, device_id_type=MESH,
        )

    def over_z(fn):
        def step(k, carry):
            d = Z // 2 + jnp.where(k % 2 == 0, k // 2, -((k + 1) // 2))
            fn((z + d) % Z)
            return carry

        lax.fori_loop(0, Z - 1, step, 0)

    def z_phase(src, dst, width):
        ssem, rsem = sem(), sem()

        def send(to):
            remote(src(to), dst, ssem, rsem, tp=2 * to + c).start()

        over_z(send)
        return ssem, rsem

    def block_wait(ref, ssem, rsem):
        return remote(ref, ref, ssem, rsem, tp=partner)

    def chip(i, width):
        return pl.ds(pl.multiple_of(i * width, 128), width)

    half = pl.ds(pl.multiple_of(8 * c, 8), 8)
    other = pl.ds(pl.multiple_of(8 * o, 8), 8)
    local = [
        pltpu.make_async_copy(kc.at[half], kbuf.at[c], lsem.at[0]),
        pltpu.make_async_copy(vc.at[half], vbuf.at[c], lsem.at[1]),
        pltpu.make_async_copy(wo, wbuf.at[c, s], lsem.at[2]),
        pltpu.make_async_copy(gw.at[0], gbuf, lsem.at[3]),
        pltpu.make_async_copy(uw.at[0], ubuf, lsem.at[4]),
        pltpu.make_async_copy(dw.at[0], dbuf, lsem.at[5]),
    ]
    for copy in local:
        copy.start()

    barrier = pltpu.get_barrier_semaphore()

    def greet(to):
        pl.semaphore_signal(barrier, inc=1, device_id={"tp": 2 * to + c}, device_id_type=MESH)

    over_z(greet)
    for d in range(1, X):
        pl.semaphore_signal(barrier, inc=1, device_id={"sub": (s + d) % X}, device_id_type=MESH)
    pl.semaphore_signal(barrier, inc=1, device_id={"tp": partner}, device_id_type=MESH)
    pl.semaphore_wait(barrier, Z - 1 + X - 1 + 1)

    swaps = [
        remote(src, dst, sem(), sem(), tp=partner)
        for src, dst in (
            (query.at[other], pq), (k_new.at[other], pk), (v_new.at[other], pv),
            (hidden.at[other], phid), (gain, pgain), (router, prouter),
            (kc.at[other], kbuf.at[c]), (vc.at[other], vbuf.at[c]), (wo, wbuf.at[c, s]),
        )
    ]
    for copy in swaps:
        copy.start()
    w_x = [
        remote(wo, wbuf.at[c, s], sem(), sem(), sub=(s + d) % X) for d in range(1, X)
    ]
    for copy in w_x:
        copy.start()
    lane = lanes((8, HD))

    def tile(value, k):
        return value[:, HD * k : HD * (k + 1)]

    def widened(*parts):
        pairs = []
        for k, part in enumerate(parts):
            small[k, : part.shape[0], : part.shape[1]] = part.astype(F32)
            pairs.append((small[k, :, :HD], small[k, :, HD:]))
        return pairs

    def chip_tiles(own, came):
        (o0, o1), (c0, c1) = widened(own, came)
        return joined(pick(c, o0, c0), pick(c, o1, c1), pick(c, c0, o0), pick(c, c1, o1))

    small[...] = jnp.zeros(small.shape, F32)
    swaps[0].wait_recv()

    q_own = chip_tiles(query[half, :], pq[...])
    qbuf[:, chip(z, CW)] = jnp.concatenate(q_own, axis=1).astype(BF16)

    own_q = qbuf.at[:, chip(z, CW)]
    q_sems = z_phase(lambda to: own_q, own_q, CW)
    for copy in swaps[1:6]:
        copy.wait_recv()
    small[...] = jnp.zeros(small.shape, F32)
    kv = [v[0] for v in widened(k_new[half, :], v_new[half, :], pk[...], pv[...])]
    kv = [pick(c, kv[0], kv[2]), pick(c, kv[1], kv[3]), pick(c, kv[2], kv[0]), pick(c, kv[3], kv[1])]
    kv = [kv[0]] + [pltpu.roll(v, 32 * (k + 1), 1) for k, v in enumerate(kv[1:])]
    kvt[...] = (kv[0] + kv[1] + kv[2] + kv[3]).astype(BF16)
    z_pair = z + 1 - 2 * (z % 2)
    kv_copy = remote(kvt, kvo, sem(), sem(), tp=2 * z_pair + c)
    kv_copy.start()

    local[0].wait()
    local[1].wait()
    swaps[6].wait_recv()
    swaps[7].wait_recv()

    all_q = block_wait(qbuf.at[:, : (Z - 1) * CW], *q_sems)
    all_q.wait_recv()

    cols = 2 * 8 * P_LOC
    group = 6
    rows = group * 8
    col = lax.broadcasted_iota(jnp.int32, (rows, cols), 1)
    row = lax.broadcasted_iota(jnp.int32, (rows, cols), 0)
    position = (2 * z + col // (8 * P_LOC)) * P_LOC + col % P_LOC
    spread = lax.broadcasted_iota(jnp.int32, (8, 16), 1)
    chosen = spread == lax.broadcasted_iota(jnp.int32, (8, 16), 0) + 8 * c

    def column(line):
        picked = jnp.where(chosen, jnp.broadcast_to(line.astype(F32), (8, 16)), 0.0)
        return jnp.sum(picked, axis=1, keepdims=True).astype(jnp.int32)

    length = jnp.broadcast_to(column(lens[...]), (8, cols))
    length = jnp.concatenate([length] * group, axis=0)
    valid = (row % 8 == (col % (8 * P_LOC)) // P_LOC) & (position < length)
    for g in range(KVH):
        at = slice(HD * g, HD * (g + 1))
        q_g = qbuf[:, group * HD * g : group * HD * (g + 1)].astype(F32)
        q_g = jnp.concatenate([tile(q_g, i) for i in range(group)], axis=0).astype(BF16)
        keys = kbuf[:, :, :, at].reshape(cols, HD)
        values = vbuf[:, :, :, at].reshape(cols, HD)
        scores = (
            lax.dot_general(q_g, keys, (((1,), (1,)), ((), ())), preferred_element_type=F32) * scale
        )
        scores = jnp.where(valid, scores, FLOOR)
        top = jnp.max(scores, axis=1, keepdims=True).astype(BF16).astype(F32)
        weights = jnp.where(valid, jnp.exp(scores - top), 0.0)
        total = jnp.sum(weights, axis=1, keepdims=True)
        summed = jnp.dot(weights.astype(BF16), values, preferred_element_type=F32)
        high = total.astype(BF16).astype(F32)
        low = total - high
        for k in range(2):
            stats = jnp.zeros((8, HD), F32)
            parts = []
            for j in range(3):
                at_row = slice(8 * (3 * k + j), 8 * (3 * k + j + 1))
                parts.append(summed[at_row])
                stats = jnp.where(lane == j, top[at_row], stats)
                stats = jnp.where(lane == 32 + j, high[at_row], stats)
                stats = jnp.where(lane == 64 + j, low[at_row], stats)
            block = jnp.concatenate(parts + [stats], axis=1).astype(BF16)
            obuf[:, 4 * HD * (2 * g + k) : 4 * HD * (2 * g + k + 1)] = block

    o_sems = z_phase(lambda to: obuf.at[:, chip(to, 4 * HD)], rbuf.at[z], 4 * HD)
    rbuf[z] = obuf[:, chip(z, 4 * HD)]
    kv_copy.wait_recv()
    t_mine, t_pair = kvt[...].astype(F32), kvo[...].astype(F32)
    even, odd = pick(z % 2, t_mine, t_pair), pick(z % 2, t_pair, t_mine)

    def quarters(shifts):
        w = [pltpu.roll(v, k, 1) if k else v for v, k in zip((even, even, odd, odd), shifts)]
        low_half = jnp.where(lane < 32, w[0], w[1])
        high_half = jnp.where(lane < 96, w[2], w[3])
        return jnp.where(lane < 64, low_half, high_half)

    key_own = quarters((0, 96, 64, 32))
    value_own = quarters((96, 64, 32, 0))
    own = jnp.zeros((8, HD), F32)
    for j in range(3):
        dot = jnp.sum(q_own[j] * key_own, axis=1, keepdims=True) * scale
        own = jnp.where(lane == j, dot, own)

    all_o = block_wait(rbuf.at[: Z - 1], *o_sems)
    all_o.wait_recv()
    tops = [rbuf[k, :, 3 * HD :].astype(F32) for k in range(Z)]
    top = own
    for part in tops:
        top = jnp.maximum(top, part)
    own_weight = jnp.where(lane < 3, jnp.exp(own - top), 0.0)
    total = own_weight
    factors = []
    for part in tops:
        factor = jnp.where(lane < 3, jnp.exp(part - top), 0.0)
        factors.append(factor)
        total = total + factor * (pltpu.roll(part, 96, 1) + pltpu.roll(part, 64, 1))
    inverse = jnp.where(lane < 3, 1.0 / jnp.where(lane < 3, total, 1.0), 0.0)
    own_weight = own_weight * inverse
    parts = []
    for j in range(3):
        value = own_weight[:, j : j + 1] * value_own
        for k in range(Z):
            factor = factors[k] * inverse
            value = value + factor[:, j : j + 1] * rbuf[k, :, HD * j : HD * (j + 1)].astype(F32)
        parts.append(value)
    abuf[:, chip(z, CW)] = jnp.concatenate(parts, axis=1).astype(BF16)

    own_a = abuf.at[:, chip(z, CW)]
    a_sems = z_phase(lambda to: own_a, own_a, CW)
    w_d = []
    for d in range(1, X):
        w_x[d - 1].wait_recv()
        block = wbuf.at[c, (s + X - d) % X]
        w_d.append(remote(block, block, sem(), sem(), tp=partner))
        w_d[-1].start()
    local[2].wait()
    swaps[8].wait_recv()

    for copy in w_d:
        copy.wait_recv()
    all_a = block_wait(abuf.at[:, : (Z - 1) * CW], *a_sems)
    all_a.wait_recv()

    for k in range(2):
        part = jnp.zeros((8, D // (2 * Z)), F32)
        for e in range(X):
            part = part + lax.dot_general(
                abuf[:, DX * e : DX * (e + 1)], wbuf[k, e],
                (((1,), (1,)), ((), ())), preferred_element_type=F32,
            )
        pbuf[k, :, HD:] = jnp.zeros((8, HD), F32)
        pbuf[k, :, : D // (2 * Z)] = part
    both = [pbuf[k] for k in range(2)]
    resid = joined(tile(both[0], 0), tile(both[0], 1), tile(both[1], 0), tile(both[1], 1))
    resid = [a + b for a, b in zip(chip_tiles(hidden[half, :], phid[...]), resid)]
    resid = jnp.concatenate(resid, axis=1)
    gains = jnp.concatenate(chip_tiles(gain[...], pgain[...]), axis=1)[0:1]
    routers = jnp.concatenate(chip_tiles(router[...], prouter[...]), axis=1)
    gained = resid * gains
    hbuf[c, s, :, chip(z, CW)] = gained.astype(BF16)
    stats = jnp.where(lane == 0, jnp.sum(resid * resid, axis=1, keepdims=True), 0.0)
    for e in range(X):
        logit = jnp.sum(gained * routers[e : e + 1], axis=1, keepdims=True)
        stats = jnp.where(lane == e + 1, logit, stats)
    tbuf[z] = stats

    own_t, own_h = tbuf.at[z], hbuf.at[c, s, :, chip(z, CW)]
    t_sems = z_phase(lambda to: own_t, own_t, HD)
    h_sems = z_phase(lambda to: own_h, own_h, CW)
    all_t = block_wait(tbuf.at[: Z - 1], *t_sems)
    all_t.wait_recv()
    sums = tbuf[0]
    for k in range(1, Z):
        sums = sums + tbuf[k]
    inv_root = 1.0 / jnp.sqrt(sums[:, 0:1] / D + 1e-05)
    irb[c, s] = jnp.broadcast_to(inv_root, (8, HD))

    hx_sems = [[(sem(), sem()) for d in range(X)] for k in range(2)]
    hd_sems = [[(sem(), sem()) for d in range(X)] for k in range(2)]

    def h_x(k, d):
        ref = (hbuf, irb)[k]
        return remote(ref.at[c, s], ref.at[c, s], *hx_sems[k][d], sub=(s + d) % X)

    def h_d(k, d):
        ref = (hbuf, irb)[k].at[c, (s + X - d) % X]
        return remote(ref, ref, *hd_sems[k][d], tp=partner)

    for d in range(1, X):
        h_x(1, d).start()
    h_d(1, 0).start()
    logits = sums * inv_root
    hot_first, hot_second = lane == column(routes[0:1, :]) + 1, lane == column(routes[1:2, :]) + 1
    l_first = jnp.sum(jnp.where(hot_first, logits, 0.0), axis=1, keepdims=True)
    l_second = jnp.sum(jnp.where(hot_second, logits, 0.0), axis=1, keepdims=True)
    w_first = 1.0 / (1.0 + jnp.exp(l_second - l_first))
    w_second = 1.0 / (1.0 + jnp.exp(l_first - l_second))
    dense = jnp.where(hot_first, w_first, 0.0) + jnp.where(hot_second, w_second, 0.0)

    def share(e):
        return jnp.sum(jnp.where(lane == e + 1, dense, 0.0), axis=1, keepdims=True)

    all_h = block_wait(hbuf.at[c, s, :, : (Z - 1) * CW], *h_sems)
    all_h.wait_recv()
    for d in range(1, X):
        h_x(0, d).start()
    h_d(0, 0).start()
    for d in range(1, X):
        for k in (1, 0):
            h_x(k, d).wait_recv()
            h_d(k, d).start()
    for d in range(X):
        for k in (1, 0):
            h_d(k, d).wait_recv()
    for copy in local[3:]:
        copy.wait()

    N = 16 * X
    F = gbuf.shape[1]
    step = 6 * HD
    gate = jnp.zeros((N, F), F32)
    up = jnp.zeros((N, F), F32)
    for k in range(0, D, step):
        left = hbuf[:, :, :, k : k + step].astype(F32).reshape(N, step).astype(BF16)
        gate = gate + jnp.dot(left, gbuf[k : k + step], preferred_element_type=F32)
        up = up + jnp.dot(left, ubuf[k : k + step], preferred_element_type=F32)
    inv = irb[...].reshape(N, HD)
    inv = jnp.concatenate([inv] * (F // HD), axis=1)
    gate, up = gate * inv, up * inv
    inner[...] = (gate / (1.0 + jnp.exp(-gate)) * up).reshape(2, N // 2, F).astype(BF16)
    order = [0] * Z
    for k in range(Z - 1):
        order[k] = Z // 2 + (k // 2 if k % 2 == 0 else -((k + 1) // 2))
    per = Z // CHUNKS
    wide = per * CW
    targets = [(z + d) % Z for d in order]
    y_copies = []
    for h in range(CHUNKS):
        for p in range(per):
            at = slice(CW * p, CW * (p + 1))
            weight = dbuf[:, chip(targets[per * h + p], CW)]
            part = jnp.dot(inner[o], weight, preferred_element_type=F32)
            ysend[h, :, :, at] = part.reshape(X, 8, CW).astype(BF16)
        y_copies.append(remote(ysend.at[h], yrecv.at[h], sem(), sem(), tp=partner))
        y_copies[-1].start()
    for h in range(CHUNKS):
        for p in range(per):
            at = slice(CW * p, CW * (p + 1))
            weight = dbuf[:, chip(targets[per * h + p], CW)]
            part = jnp.dot(inner[c], weight, preferred_element_type=F32)
            ymine[h, :, :, at] = part.reshape(X, 8, CW)
    x_copies = []
    x_sems = [(sem(), sem()) for h in range(CHUNKS)]
    for h in range(CHUNKS):
        y_copies[h].wait_recv()
        for d in range(1, X):
            to = (s + d) % X
            xsend[h, d - 1] = (ymine[h, to] + yrecv[h, to].astype(F32)).astype(BF16)
            copy = remote(xsend.at[h, d - 1], xrecv.at[h, d - 1], *x_sems[h], sub=to)
            copy.start()
        x_copies.append(block_wait(xrecv.at[h], *x_sems[h]))
        acc[h] = share(s) * (ymine[h, s] + yrecv[h, s].astype(F32))
    z_sems = sem(), sem()
    for h in range(CHUNKS):
        x_copies[h].wait_recv()
        total = acc[h]
        for d in range(1, X):
            total = total + share((s + X - d) % X) * xrecv[h, d - 1].astype(F32)
        acc[h] = total
        zsend[h] = total.astype(BF16)
        for p in range(per):
            k = per * h + p
            if k < Z - 1:
                at = slice(CW * p, CW * (p + 1))
                remote(
                    zsend.at[h, :, at], zrecv.at[k], *z_sems, tp=2 * targets[k] + c
                ).start()
    result = resid + acc[CHUNKS - 1, :, (per - 1) * CW :]
    all_z = block_wait(zrecv, *z_sems)
    all_z.wait_recv()
    for k in range(Z - 1):
        result = result + zrecv[k].astype(F32)

    r1, r2 = pltpu.roll(tile(result, 1), 64, 1), pltpu.roll(tile(result, 2), 64, 1)
    v_first = result[:, : 2 * HD]
    v_second = jnp.concatenate([jnp.where(lane < 64, r1, r2), r2], axis=1)
    fsend[...] = pick(c, v_second, v_first).astype(BF16)
    f_copy = remote(fsend, frecv, sem(), sem(), tp=partner)
    f_copy.start()
    kept = pick(c, v_first, v_second)

    for copy in (all_q, all_o, all_a, all_h, all_t, all_z, kv_copy):
        copy.wait_send()
    for copy in swaps + w_x + w_d + y_copies + x_copies:
        copy.wait_send()
    for k in range(2):
        for d in range(1, X):
            h_x(k, d).wait_send()
        for d in range(X):
            h_d(k, d).wait_send()
    f_copy.wait()
    came = frecv[...].astype(F32)
    whole = jnp.concatenate([pick(c, kept, came), pick(c, came, kept)], axis=0)
    out[...] = whole[:, : D // (2 * Z)].astype(BF16)


def on_device(
    Z, X,
    hidden_in, query, key_new, value_new, key_cache, value_cache, lengths,
    out_weight, norm_gain, router_weight, routes, gate_weight, up_weight, down_weight,
):
    width = hidden_in.shape[1]
    D = width * 2 * Z
    P_LOC = key_cache.shape[1]
    F = gate_weight.shape[2]
    CW = 3 * HD
    KV = key_new.shape[1]
    W = D // CHUNKS
    vm = pl.BlockSpec(memory_space=pltpu.VMEM)
    anywhere = pl.BlockSpec(memory_space=pl.ANY)
    dma = pltpu.SemaphoreType.DMA
    V = pltpu.VMEM
    scratch = [
        V((8, width), BF16), V((8, width), BF16), V((8, KV), BF16), V((8, KV), BF16),
        V((1, width), BF16), V((X, width), BF16), V((4, 8, 2 * HD), F32),
        V((2, 8, P_LOC, key_cache.shape[2]), BF16), V((2, 8, P_LOC, key_cache.shape[2]), BF16),
        V((2, X, width, D // X), BF16),
        V((D, F), BF16), V((D, F), BF16), V((F, D), BF16),
        V((8, HD), BF16), V((8, HD), BF16),
        V((8, D), BF16),
        V((8, Z * 4 * HD), BF16), V((Z, 8, 4 * HD), BF16),
        V((8, D), BF16), V((2, 8, 2 * HD), F32),
        V((2, X, 8, D), BF16), V((Z, 8, HD), F32), V((2, X, 8, HD), F32),
        V((2, 8 * X, F), BF16),
        V((CHUNKS, X, 8, W), BF16), V((CHUNKS, X, 8, W), BF16), V((CHUNKS, X, 8, W), F32),
        V((CHUNKS, X - 1, 8, W), BF16), V((CHUNKS, X - 1, 8, W), BF16),
        V((CHUNKS, 8, W), F32), V((CHUNKS, 8, W), BF16), V((Z - 1, 8, CW), BF16),
        V((8, 2 * HD), BF16), V((8, 2 * HD), BF16),
        dma((6,)), dma((SEMAPHORES,)),
    ]
    return pl.pallas_call(
        functools.partial(layer, Z, X, D, P_LOC),
        out_shape=jax.ShapeDtypeStruct(hidden_in.shape, BF16),
        in_specs=[vm] * 8 + [anywhere] * 6,
        out_specs=vm,
        scratch_shapes=scratch,
        compiler_params=pltpu.CompilerParams(
            collective_id=0, has_side_effects=True, vmem_limit_bytes=56 * 1024 * 1024
        ),
        name="decode_layer",
    )(
        hidden_in, query, key_new, value_new, lengths[None], routes.T, norm_gain[None],
        router_weight.T, key_cache, value_cache, out_weight.T, gate_weight, up_weight, down_weight,
    )


def solution(mesh):
    Z, X = mesh.shape["tp"] // 2, mesh.shape["sub"]
    rows = P(("rep", "sub"), "tp")
    return jax.shard_map(
        functools.partial(on_device, Z, X),
        mesh=mesh,
        in_specs=(
            rows, rows, rows, rows,
            P(("rep", "sub"), "tp", None), P(("rep", "sub"), "tp", None), P(("rep", "sub")),
            P("sub", "tp"), P("tp"), P("tp", None), P(("rep", "sub"), None),
            P("sub", None, "tp"), P("sub", None, "tp"), P("sub", "tp", None),
        ),
        out_specs=rows,
        check_vma=False,
    )
```

time: 112 us -> 99.4 us (0.89)
  Pallas kernels: 102 us -> 96.6 us
  local copies, waits for them, and re-layouts: 6.84 us -> 2.52 us
  other arithmetic: 2.71 us -> 0 us
    pallas_call x1, Pallas kernels: 102 us -> 96.6 us  [on_device(): pl.pallas_call(functools.partial(layer, Z, X, D, P_LOC), out_shape=jax.Sh...]
    unnamed x3 -> x1, local copies, waits for them, and re-layouts: 4.86 us -> 1.3 us
    reshape x1 -> x0, other arithmetic: 1.43 us -> none  [on_device(): pk = jnp.pad(pk, ((0, 0), (0, 4 * HD - pk.shape[1]))).reshape(2, 8, 4 * HD)]
    pad x1 -> x0, other arithmetic: 1.29 us -> none  [on_device(): gr = jnp.pad(gr, ((0, 8 - gr.shape[0]), (0, 2 * HD - width)))]
where the time goes in v2:
time: 99.4 us; the launch traced here: 99.2 us
  Pallas kernels  96.6 us (97%)
  local copies, waits for them, and re-layouts  2.52 us (3%)
    pallas_call x1, Pallas kernels, on_device(): pl.pallas_call(functools.partial(layer, Z, X, D, P_LOC), out_shape=jax.Sh...  96.6 us

profile of v2, /device:TPU:33, one launch (start us, length us, event | category | flops | bytes accessed | tf_op | source)
XLA Modules:
  0.0 99.2 jit_solution(10588306927901269733)
XLA Ops:
  0.0 1.2 %broadcast_in_dim.7.gain = bf16[1,192]{1,0:T(2,128)(2,1)} reshape(bf16[192]{0:T(256)(128)(2,1)} %param.22) | data formatting | bytes 768 | tf_op jit(solution)/shard_map/broadcast_in_dim | solution.py:480
  1.2 96.6 %decode_layer.1 = bf16[16,192]{1,0:T(8,128)(2,1)} custom-call(bf16[16,192]{1,0:T(8,128)(2,1)} %hidden.1, bf16[16,192]{1,0:T(8,128)(2,1)} %query.1, bf16[16,32]{1,0:T(8,128)(2,1)} %k_new.1, bf16[16,32]{1,0:T(8,128)(2,1)} %v_new.1, s32[1,16]{1,0:T(1,128)} %bitcast.7, s32[2,16]{1,0:T(2,128)} %bitcast.6, bf16[1,192]{1,0:T(2,128)(2,1)} %broadcast_in_dim.7.gain, ...), custom_call_target="tpu_custom_call" | custom-call | tf_op jit(solution)/shard_map/decode_layer/pallas_call | solution.py:469
  97.9 1.3 %copy.16 = bf16[16,192]{1,0:T(8,128)(2,1)} copy(bf16[16,192]{1,0:T(8,128)(2,1)} %decode_layer.1) | data formatting | bytes 12288

commit v3 on v2

--- a/solution.py
+++ b/solution.py
@@ -13,7 +13,13 @@
 MESH = pl.DeviceIdType.MESH
 FLOOR = -1e30
 CHUNKS = 4
-SEMAPHORES = 96
+SEMAPHORES = 112
+
+
+def far_first(count):
+    middle = count // 2
+    far = [middle + (k // 2 if k % 2 == 0 else -((k + 1) // 2)) for k in range(count - 1)]
+    return far + [0]
 
 
 def lanes(shape):
@@ -36,9 +42,9 @@
     out,
     phid, pq, pk, pv, pgain, prouter, small,
     kbuf, vbuf, wbuf, gbuf, ubuf, dbuf,
-    kvt, kvo, qbuf, obuf, rbuf, abuf, pbuf,
+    kvt, kvo, base, qbuf, obuf, rbuf, abuf, pbuf,
     hbuf, tbuf, irb, inner, ysend, yrecv, ymine, xsend, xrecv, acc, zsend, zrecv, fsend, frecv,
-    lsem, sems,
+    lsem, sems, tokens,
 ):
     t = lax.axis_index("tp")
     s = lax.axis_index("sub")
@@ -50,6 +56,10 @@
     KVH = Z // 2
     DX = D // X
     taken = iter(range(SEMAPHORES))
+    order = far_first(Z)
+    targets = [(z + d) % Z for d in order]
+    sources = [(z + Z - d) % Z for d in order]
+    per = Z // CHUNKS
     scale = 1.0 / HD**0.5
 
     def sem():
@@ -77,6 +87,17 @@
 
         over_z(send)
         return ssem, rsem
+
+    def spread(ref):
+        pairs = [(sem(), sem()) for h in range(CHUNKS)]
+        for k in range(Z - 1):
+            h, at = k // per, pl.ds(CW * (k % per), CW)
+            remote(
+                ref.at[CHUNKS - 1, :, (per - 1) * CW :], ref.at[h, :, at], *pairs[h],
+                tp=2 * targets[k] + c,
+            ).start()
+        waits = [block_wait(ref.at[h], *pairs[h]) for h in range(CHUNKS - 1)]
+        return waits + [block_wait(ref.at[CHUNKS - 1, :, : (per - 1) * CW], *pairs[-1])]
 
     def block_wait(ref, ssem, rsem):
         return remote(ref, ref, ssem, rsem, tp=partner)
@@ -99,14 +120,23 @@
 
     barrier = pltpu.get_barrier_semaphore()
 
-    def greet(to):
-        pl.semaphore_signal(barrier, inc=1, device_id={"tp": 2 * to + c}, device_id_type=MESH)
-
-    over_z(greet)
+    def signal(what, **where):
+        pl.semaphore_signal(what, inc=1, device_id=where, device_id_type=MESH)
+
+    def around(d):
+        return 2 * ((z + d) % Z) + c
+
+    near = [d for k in range(Z // 4, 0, -1) for d in (k, -k)]
+    for d in near:
+        signal(barrier, tp=around(d))
     for d in range(1, X):
-        pl.semaphore_signal(barrier, inc=1, device_id={"sub": (s + d) % X}, device_id_type=MESH)
-    pl.semaphore_signal(barrier, inc=1, device_id={"tp": partner}, device_id_type=MESH)
-    pl.semaphore_wait(barrier, Z - 1 + X - 1 + 1)
+        signal(barrier, sub=(s + d) % X)
+    signal(barrier, tp=partner)
+    pl.semaphore_wait(barrier, len(near) + X - 1 + 1)
+
+    def tell():
+        signal(tokens.at[0], tp=around(Z // 4))
+        signal(tokens.at[1], tp=around(-(Z // 4)))
 
     swaps = [
         remote(src, dst, sem(), sem(), tp=partner)
@@ -118,11 +148,13 @@
     ]
     for copy in swaps:
         copy.start()
-    w_x = [
-        remote(wo, wbuf.at[c, s], sem(), sem(), sub=(s + d) % X) for d in range(1, X)
-    ]
-    for copy in w_x:
+    ways = (1, X - 1) if X == 4 else range(1, X)
+    w_x = {
+        d: remote(wo, wbuf.at[c, s], sem(), sem(), sub=(s + d) % X) for d in ways
+    }
+    for copy in w_x.values():
         copy.start()
+    tell()
     lane = lanes((8, HD))
 
     def tile(value, k):
@@ -146,7 +178,15 @@
     qbuf[:, chip(z, CW)] = jnp.concatenate(q_own, axis=1).astype(BF16)
 
     own_q = qbuf.at[:, chip(z, CW)]
-    q_sems = z_phase(lambda to: own_q, own_q, CW)
+    bands = Z // 4 + 1
+    q_sems = [(sem(), sem()) for b in range(bands)]
+    pl.semaphore_wait(tokens.at[0], 1)
+    pl.semaphore_wait(tokens.at[1], 1)
+    for d in order[:-1]:
+        band = min(d, Z - d) // 2
+        remote(own_q, own_q, *q_sems[band], tp=around(d)).start()
+    sizes = [sum(min(d, Z - d) // 2 == b for d in range(1, Z)) for b in range(bands)]
+    q_waits = [block_wait(qbuf.at[:, : n * CW], *q_sems[b]) for b, n in enumerate(sizes)]
     for copy in swaps[1:6]:
         copy.wait_recv()
     small[...] = jnp.zeros(small.shape, F32)
@@ -158,13 +198,13 @@
     kv_copy = remote(kvt, kvo, sem(), sem(), tp=2 * z_pair + c)
     kv_copy.start()
 
+    base[0] = jnp.concatenate(chip_tiles(hidden[half, :], phid[...]), axis=1)
+    base[1] = jnp.concatenate(chip_tiles(gain[...].reshape(1, -1), pgain[...].reshape(1, -1)), axis=1)
+    base[2] = jnp.concatenate(chip_tiles(router[...], prouter[...]), axis=1)
     local[0].wait()
     local[1].wait()
     swaps[6].wait_recv()
     swaps[7].wait_recv()
-
-    all_q = block_wait(qbuf.at[:, : (Z - 1) * CW], *q_sems)
-    all_q.wait_recv()
 
     cols = 2 * 8 * P_LOC
     group = 6
@@ -172,8 +212,8 @@
     col = lax.broadcasted_iota(jnp.int32, (rows, cols), 1)
     row = lax.broadcasted_iota(jnp.int32, (rows, cols), 0)
     position = (2 * z + col // (8 * P_LOC)) * P_LOC + col % P_LOC
-    spread = lax.broadcasted_iota(jnp.int32, (8, 16), 1)
-    chosen = spread == lax.broadcasted_iota(jnp.int32, (8, 16), 0) + 8 * c
+    slot = lax.broadcasted_iota(jnp.int32, (8, 16), 1)
+    chosen = slot == lax.broadcasted_iota(jnp.int32, (8, 16), 0) + 8 * c
 
     def column(line):
         picked = jnp.where(chosen, jnp.broadcast_to(line.astype(F32), (8, 16)), 0.0)
@@ -182,9 +222,20 @@
     length = jnp.broadcast_to(column(lens[...]), (8, cols))
     length = jnp.concatenate([length] * group, axis=0)
     valid = (row % 8 == (col % (8 * P_LOC)) // P_LOC) & (position < length)
-    for g in range(KVH):
-        at = slice(HD * g, HD * (g + 1))
-        q_g = qbuf[:, group * HD * g : group * HD * (g + 1)].astype(F32)
+    o_sems = sem(), sem()
+
+    def send_o(to):
+        remote(obuf.at[:, chip(to, 4 * HD)], rbuf.at[z], *o_sems, tp=2 * to + c).start()
+
+    ready = []
+    for turn in far_first(KVH)[::-1]:
+        band = min(turn, KVH - turn)
+        if band not in ready:
+            q_waits[band].wait_recv()
+            ready.append(band)
+        g = (z // 2 + turn) % KVH
+        at = chip(g, HD)
+        q_g = qbuf[:, chip(g, group * HD)].astype(F32)
         q_g = jnp.concatenate([tile(q_g, i) for i in range(group)], axis=0).astype(BF16)
         keys = kbuf[:, :, :, at].reshape(cols, HD)
         values = vbuf[:, :, :, at].reshape(cols, HD)
@@ -208,9 +259,28 @@
                 stats = jnp.where(lane == 32 + j, high[at_row], stats)
                 stats = jnp.where(lane == 64 + j, low[at_row], stats)
             block = jnp.concatenate(parts + [stats], axis=1).astype(BF16)
-            obuf[:, 4 * HD * (2 * g + k) : 4 * HD * (2 * g + k + 1)] = block
-
-    o_sems = z_phase(lambda to: obuf.at[:, chip(to, 4 * HD)], rbuf.at[z], 4 * HD)
+            obuf[:, chip(2 * g + k, 4 * HD)] = block
+        if turn:
+            send_o(2 * g)
+            send_o(2 * g + 1)
+        else:
+            send_o(z_pair)
+    w_d, w_r = [], []
+    top_half = wbuf.shape[2] // 2
+
+    def handed_on(ref):
+        copy = remote(ref, ref, sem(), sem(), tp=partner)
+        copy.start()
+        return copy
+
+    for d, copy in w_x.items():
+        copy.wait_recv()
+        block = wbuf.at[c, (s + X - d) % X]
+        if X == 4:
+            part = block.at[pl.ds(0 if d == 1 else top_half, top_half)]
+            w_r.append(remote(part, part, sem(), sem(), sub=(s + d) % X))
+            w_r[-1].start()
+        w_d.append(handed_on(block))
     rbuf[z] = obuf[:, chip(z, 4 * HD)]
     kv_copy.wait_recv()
     t_mine, t_pair = kvt[...].astype(F32), kvo[...].astype(F32)
@@ -251,72 +321,68 @@
             factor = factors[k] * inverse
             value = value + factor[:, j : j + 1] * rbuf[k, :, HD * j : HD * (j + 1)].astype(F32)
         parts.append(value)
-    abuf[:, chip(z, CW)] = jnp.concatenate(parts, axis=1).astype(BF16)
-
-    own_a = abuf.at[:, chip(z, CW)]
-    a_sems = z_phase(lambda to: own_a, own_a, CW)
-    w_d = []
-    for d in range(1, X):
-        w_x[d - 1].wait_recv()
-        block = wbuf.at[c, (s + X - d) % X]
-        w_d.append(remote(block, block, sem(), sem(), tp=partner))
-        w_d[-1].start()
+    abuf[CHUNKS - 1, :, (per - 1) * CW :] = jnp.concatenate(parts, axis=1).astype(BF16)
+    a_waits = spread(abuf)
+    if X == 4:
+        block = wbuf.at[c, (s + 2) % X]
+        for copy in w_r:
+            copy.wait_recv()
+        w_d.append(handed_on(block))
     local[2].wait()
     swaps[8].wait_recv()
 
     for copy in w_d:
         copy.wait_recv()
-    all_a = block_wait(abuf.at[:, : (Z - 1) * CW], *a_sems)
-    all_a.wait_recv()
-
+    sums = [jnp.zeros((8, D // (2 * Z)), F32) for k in range(2)]
+    for h in reversed(range(CHUNKS)):
+        a_waits[h].wait_recv()
+        for p in range(per):
+            source = sources[per * h + p]
+            e, at = source // (Z // X), chip(source % (Z // X), CW)
+            for k in range(2):
+                sums[k] = sums[k] + lax.dot_general(
+                    abuf[h, :, CW * p : CW * (p + 1)], wbuf[k, e, :, at],
+                    (((1,), (1,)), ((), ())), preferred_element_type=F32,
+                )
     for k in range(2):
-        part = jnp.zeros((8, D // (2 * Z)), F32)
-        for e in range(X):
-            part = part + lax.dot_general(
-                abuf[:, DX * e : DX * (e + 1)], wbuf[k, e],
-                (((1,), (1,)), ((), ())), preferred_element_type=F32,
-            )
         pbuf[k, :, HD:] = jnp.zeros((8, HD), F32)
-        pbuf[k, :, : D // (2 * Z)] = part
+        pbuf[k, :, : D // (2 * Z)] = sums[k]
     both = [pbuf[k] for k in range(2)]
     resid = joined(tile(both[0], 0), tile(both[0], 1), tile(both[1], 0), tile(both[1], 1))
-    resid = [a + b for a, b in zip(chip_tiles(hidden[half, :], phid[...]), resid)]
-    resid = jnp.concatenate(resid, axis=1)
-    gains = jnp.concatenate(chip_tiles(gain[...], pgain[...]), axis=1)[0:1]
-    routers = jnp.concatenate(chip_tiles(router[...], prouter[...]), axis=1)
+    resid = base[0] + jnp.concatenate(resid, axis=1)
+    gains, routers = base[1, 0:1], base[2]
     gained = resid * gains
-    hbuf[c, s, :, chip(z, CW)] = gained.astype(BF16)
     stats = jnp.where(lane == 0, jnp.sum(resid * resid, axis=1, keepdims=True), 0.0)
     for e in range(X):
         logit = jnp.sum(gained * routers[e : e + 1], axis=1, keepdims=True)
         stats = jnp.where(lane == e + 1, logit, stats)
-    tbuf[z] = stats
-
-    own_t, own_h = tbuf.at[z], hbuf.at[c, s, :, chip(z, CW)]
+    high = stats.astype(BF16).astype(F32)
+    middle = (stats - high).astype(BF16).astype(F32)
+    low = stats - high - middle
+    tbuf[z] = (high + pltpu.roll(middle, 32, 1) + pltpu.roll(low, 64, 1)).astype(BF16)
+    own_t = tbuf.at[z]
     t_sems = z_phase(lambda to: own_t, own_t, HD)
-    h_sems = z_phase(lambda to: own_h, own_h, CW)
+    own_h = hbuf.at[c, :, 0]
+    own_h[CHUNKS - 1, :, (per - 1) * CW :] = gained.astype(BF16)
+    h_waits = spread(own_h)
+    hx_sems = [(sem(), sem()) for h in range(CHUNKS)]
+    x_waits = [block_wait(hbuf.at[c, h, 1:], *hx_sems[h]) for h in range(CHUNKS)]
+    for h in reversed(range(CHUNKS)):
+        h_waits[h].wait_recv()
+        for d in range(1, X):
+            remote(hbuf.at[c, h, 0], hbuf.at[c, h, d], *hx_sems[h], sub=(s + d) % X).start()
     all_t = block_wait(tbuf.at[: Z - 1], *t_sems)
     all_t.wait_recv()
-    sums = tbuf[0]
+    sums = tbuf[0].astype(F32)
     for k in range(1, Z):
-        sums = sums + tbuf[k]
+        sums = sums + tbuf[k].astype(F32)
+    sums = sums + pltpu.roll(sums, 96, 1) + pltpu.roll(sums, 64, 1)
     inv_root = 1.0 / jnp.sqrt(sums[:, 0:1] / D + 1e-05)
-    irb[c, s] = jnp.broadcast_to(inv_root, (8, HD))
-
-    hx_sems = [[(sem(), sem()) for d in range(X)] for k in range(2)]
-    hd_sems = [[(sem(), sem()) for d in range(X)] for k in range(2)]
-
-    def h_x(k, d):
-        ref = (hbuf, irb)[k]
-        return remote(ref.at[c, s], ref.at[c, s], *hx_sems[k][d], sub=(s + d) % X)
-
-    def h_d(k, d):
-        ref = (hbuf, irb)[k].at[c, (s + X - d) % X]
-        return remote(ref, ref, *hd_sems[k][d], tp=partner)
-
+    irb[c, 0] = jnp.broadcast_to(inv_root, (8, HD))
+    ix_sems = sem(), sem()
     for d in range(1, X):
-        h_x(1, d).start()
-    h_d(1, 0).start()
+        remote(irb.at[c, 0], irb.at[c, d], *ix_sems, sub=(s + d) % X).start()
+    ix_wait = block_wait(irb.at[c, 1:], *ix_sems)
     logits = sums * inv_root
     hot_first, hot_second = lane == column(routes[0:1, :]) + 1, lane == column(routes[1:2, :]) + 1
     l_first = jnp.sum(jnp.where(hot_first, logits, 0.0), axis=1, keepdims=True)
@@ -328,40 +394,38 @@
     def share(e):
         return jnp.sum(jnp.where(lane == e + 1, dense, 0.0), axis=1, keepdims=True)
 
-    all_h = block_wait(hbuf.at[c, s, :, : (Z - 1) * CW], *h_sems)
-    all_h.wait_recv()
-    for d in range(1, X):
-        h_x(0, d).start()
-    h_d(0, 0).start()
-    for d in range(1, X):
-        for k in (1, 0):
-            h_x(k, d).wait_recv()
-            h_d(k, d).start()
-    for d in range(X):
-        for k in (1, 0):
-            h_d(k, d).wait_recv()
+    N = 16 * X
+    F = gbuf.shape[1]
     for copy in local[3:]:
         copy.wait()
-
-    N = 16 * X
-    F = gbuf.shape[1]
-    step = 6 * HD
     gate = jnp.zeros((N, F), F32)
     up = jnp.zeros((N, F), F32)
-    for k in range(0, D, step):
-        left = hbuf[:, :, :, k : k + step].astype(F32).reshape(N, step).astype(BF16)
-        gate = gate + jnp.dot(left, gbuf[k : k + step], preferred_element_type=F32)
-        up = up + jnp.dot(left, ubuf[k : k + step], preferred_element_type=F32)
+    d_copies = {}
+
+    def columns(h, gate, up):
+        d_copies[h].wait_recv()
+        rows_in = hbuf[:, h].astype(F32).reshape(N, per * CW).astype(BF16)
+        for p in range(per):
+            left = rows_in[:, CW * p : CW * (p + 1)]
+            at = chip(sources[per * h + p], CW)
+            gate = gate + jnp.dot(left, gbuf[at, :], preferred_element_type=F32)
+            up = up + jnp.dot(left, ubuf[at, :], preferred_element_type=F32)
+        return gate, up
+
+    for h in reversed(range(CHUNKS)):
+        x_waits[h].wait_recv()
+        d_copies[h] = handed_on(hbuf.at[c, h])
+        if h == 0:
+            ix_wait.wait_recv()
+            i_copy = handed_on(irb.at[c])
+        if h + 1 < CHUNKS:
+            gate, up = columns(h + 1, gate, up)
+    gate, up = columns(0, gate, up)
+    i_copy.wait_recv()
     inv = irb[...].reshape(N, HD)
     inv = jnp.concatenate([inv] * (F // HD), axis=1)
     gate, up = gate * inv, up * inv
     inner[...] = (gate / (1.0 + jnp.exp(-gate)) * up).reshape(2, N // 2, F).astype(BF16)
-    order = [0] * Z
-    for k in range(Z - 1):
-        order[k] = Z // 2 + (k // 2 if k % 2 == 0 else -((k + 1) // 2))
-    per = Z // CHUNKS
-    wide = per * CW
-    targets = [(z + d) % Z for d in order]
     y_copies = []
     for h in range(CHUNKS):
         for p in range(per):
@@ -371,29 +435,28 @@
             ysend[h, :, :, at] = part.reshape(X, 8, CW).astype(BF16)
         y_copies.append(remote(ysend.at[h], yrecv.at[h], sem(), sem(), tp=partner))
         y_copies[-1].start()
+    x_copies = []
+    x_sems = [(sem(), sem()) for h in range(CHUNKS)]
     for h in range(CHUNKS):
         for p in range(per):
             at = slice(CW * p, CW * (p + 1))
             weight = dbuf[:, chip(targets[per * h + p], CW)]
             part = jnp.dot(inner[c], weight, preferred_element_type=F32)
             ymine[h, :, :, at] = part.reshape(X, 8, CW)
-    x_copies = []
-    x_sems = [(sem(), sem()) for h in range(CHUNKS)]
-    for h in range(CHUNKS):
         y_copies[h].wait_recv()
         for d in range(1, X):
-            to = (s + d) % X
-            xsend[h, d - 1] = (ymine[h, to] + yrecv[h, to].astype(F32)).astype(BF16)
+            to = (s + X - d) % X
+            xsend[h, d - 1] = (ymine[h, d] + yrecv[h, d].astype(F32)).astype(BF16)
             copy = remote(xsend.at[h, d - 1], xrecv.at[h, d - 1], *x_sems[h], sub=to)
             copy.start()
         x_copies.append(block_wait(xrecv.at[h], *x_sems[h]))
-        acc[h] = share(s) * (ymine[h, s] + yrecv[h, s].astype(F32))
+        acc[h] = share(s) * (ymine[h, 0] + yrecv[h, 0].astype(F32))
     z_sems = sem(), sem()
     for h in range(CHUNKS):
         x_copies[h].wait_recv()
         total = acc[h]
         for d in range(1, X):
-            total = total + share((s + X - d) % X) * xrecv[h, d - 1].astype(F32)
+            total = total + share((s + d) % X) * xrecv[h, d - 1].astype(F32)
         acc[h] = total
         zsend[h] = total.astype(BF16)
         for p in range(per):
@@ -417,15 +480,10 @@
     f_copy.start()
     kept = pick(c, v_first, v_second)
 
-    for copy in (all_q, all_o, all_a, all_h, all_t, all_z, kv_copy):
+    for copy in [all_o, all_t, all_z, kv_copy, ix_wait, i_copy] + a_waits + h_waits + q_waits:
         copy.wait_send()
-    for copy in swaps + w_x + w_d + y_copies + x_copies:
+    for copy in swaps + list(w_x.values()) + w_r + w_d + y_copies + x_copies + x_waits + list(d_copies.values()):
         copy.wait_send()
-    for k in range(2):
-        for d in range(1, X):
-            h_x(k, d).wait_send()
-        for d in range(X):
-            h_d(k, d).wait_send()
     f_copy.wait()
     came = frecv[...].astype(F32)
     whole = jnp.concatenate([pick(c, kept, came), pick(c, came, kept)], axis=0)
@@ -450,21 +508,21 @@
     V = pltpu.VMEM
     scratch = [
         V((8, width), BF16), V((8, width), BF16), V((8, KV), BF16), V((8, KV), BF16),
-        V((1, width), BF16), V((X, width), BF16), V((4, 8, 2 * HD), F32),
+        V((width,), BF16), V((X, width), BF16), V((4, 8, 2 * HD), F32),
         V((2, 8, P_LOC, key_cache.shape[2]), BF16), V((2, 8, P_LOC, key_cache.shape[2]), BF16),
         V((2, X, width, D // X), BF16),
         V((D, F), BF16), V((D, F), BF16), V((F, D), BF16),
-        V((8, HD), BF16), V((8, HD), BF16),
+        V((8, HD), BF16), V((8, HD), BF16), V((3, 8, CW), F32),
         V((8, D), BF16),
         V((8, Z * 4 * HD), BF16), V((Z, 8, 4 * HD), BF16),
-        V((8, D), BF16), V((2, 8, 2 * HD), F32),
-        V((2, X, 8, D), BF16), V((Z, 8, HD), F32), V((2, X, 8, HD), F32),
+        V((CHUNKS, 8, W), BF16), V((2, 8, 2 * HD), F32),
+        V((2, CHUNKS, X, 8, W), BF16), V((Z, 8, HD), BF16), V((2, X, 8, HD), F32),
         V((2, 8 * X, F), BF16),
         V((CHUNKS, X, 8, W), BF16), V((CHUNKS, X, 8, W), BF16), V((CHUNKS, X, 8, W), F32),
         V((CHUNKS, X - 1, 8, W), BF16), V((CHUNKS, X - 1, 8, W), BF16),
         V((CHUNKS, 8, W), F32), V((CHUNKS, 8, W), BF16), V((Z - 1, 8, CW), BF16),
         V((8, 2 * HD), BF16), V((8, 2 * HD), BF16),
-        dma((6,)), dma((SEMAPHORES,)),
+        dma((6,)), dma((SEMAPHORES,)), pltpu.SemaphoreType.REGULAR((2,)),
     ]
     return pl.pallas_call(
         functools.partial(layer, Z, X, D, P_LOC),
@@ -477,7 +535,7 @@
         ),
         name="decode_layer",
     )(
-        hidden_in, query, key_new, value_new, lengths[None], routes.T, norm_gain[None],
+        hidden_in, query, key_new, value_new, lengths[None], routes.T, norm_gain,
         router_weight.T, key_cache, value_cache, out_weight.T, gate_weight, up_weight, down_weight,
     )
 

time: 99.4 us -> 87.3 us (0.88)
  Pallas kernels: 96.6 us -> 85.8 us
  local copies, waits for them, and re-layouts: 2.52 us -> 1.3 us
    pallas_call x1, Pallas kernels: 96.6 us -> 85.8 us  [on_device(): pl.pallas_call(functools.partial(layer, Z, X, D, P_LOC), out_shape=jax.Sh...]
    broadcast_in_dim x1 -> x0, local copies, waits for them, and re-layouts: 1.22 us -> none  [on_device(): norm_gain[None]]
where the time goes in v3:
time: 87.3 us; the launch traced here: 87.1 us
  Pallas kernels  85.8 us (98%)
  local copies, waits for them, and re-layouts  1.3 us (1%)
    pallas_call x1, Pallas kernels, on_device(): pl.pallas_call(functools.partial(layer, Z, X, D, P_LOC), out_shape=jax.Sh...  85.8 us

profile of v3, /device:TPU:33, one launch (start us, length us, event | category | flops | bytes accessed | tf_op | source)
XLA Modules:
  0.0 87.1 jit_solution(5394831518733027907)
XLA Ops:
  0.0 85.8 %decode_layer.1 = bf16[16,192]{1,0:T(8,128)(2,1)} custom-call(bf16[16,192]{1,0:T(8,128)(2,1)} %hidden.1, bf16[16,192]{1,0:T(8,128)(2,1)} %query.1, bf16[16,32]{1,0:T(8,128)(2,1)} %k_new.1, bf16[16,32]{1,0:T(8,128)(2,1)} %v_new.1, s32[1,16]{1,0:T(1,128)} %bitcast.7, s32[2,16]{1,0:T(2,128)} %bitcast.6, bf16[192]{0:T(256)(128)(2,1)} %gain.1, ...), custom_call_target="tpu_custom_call" | custom-call | tf_op jit(solution)/shard_map/decode_layer/pallas_call | solution.py:527
  85.8 1.3 %copy.16 = bf16[16,192]{1,0:T(8,128)(2,1)} copy(bf16[16,192]{1,0:T(8,128)(2,1)} %decode_layer.1) | data formatting | bytes 12288
